TPU v7x, 32 devices: a whole 2x2x4 slice. The times are simulated.
32 devices in a mesh: gx: 4 (over z), gy: 4 (over y, x), gz: 2 (over core).
Axes of the slice: x: 2, y: 2, z: 4, core: 2. Of those that a mesh axis runs over, the one named last changes fastest.
Arguments:
- potential: float32 [16, 96, 512], P('gz', 'gx', 'gy'), may hold values from -6 to 6
- tissue_mask: int32 [16, 96, 512], P('gz', 'gx', 'gy'), may hold values from 0 to 2, as said below
- layer_index: int32 [16], P('gz'), may hold values from 0 to 15
- source: float32 [16, 96, 512], P('gz', 'gx', 'gy'), may hold values from -6 to 6
Outputs:
- phi_e: float32 [16, 96, 512], P('gz', 'gx', 'gy')
- residual: float32 [16, 96, 512], P('gz', 'gx', 'gy')
Inputs may be any that keep to these rules, and one draw needn't show every extreme that they name: `tissue_mask`: 0 marks cells outside every medium, 1 bath, 2 tissue.
All inputs are finite; a program needn't handle non-finite values.
Results may differ from a plain program's by a relative error of at most 0.0003.
Values sent between devices are 32-bit elements; how exact they have to be, the bound alone decides.
A program may use at most 128 MiB of HBM per device.

v0:
```python
import math

import jax
import jax.numpy as jnp
from jax import lax
from jax.sharding import PartitionSpec as P

ITERS = 8
LAYERS = 16


OFFSETS = [
    (0, 1, 0),
    (0, 0, 1),
    (1, 0, 0),
    (0, 1, 1),
    (0, 1, -1),
    (1, 1, 0),
    (-1, 1, 0),
    (1, 0, 1),
    (-1, 0, 1),
]
bulk_long = 7.99
bulk_trans = 2.55
intra_long = 1.74
intra_trans = 0.19
bath_sigma = 5.0


def padded(value, sides, width):
    for axis, dim in sides:
        count, length = (lax.axis_size(axis), value.shape[dim])
        up = [(i, (i + 1) % count) for i in range(count - 1)]
        down = [(j, i) for i, j in up]
        last = lax.slice_in_dim(value, length - width, length, axis=dim)
        first = lax.slice_in_dim(value, 0, width, axis=dim)
        before = lax.ppermute(last, axis, up)
        after = lax.ppermute(first, axis, down)
        value = jnp.concatenate([before, value, after], axis=dim)
    return value


def tensor_table(layers, longitudinal, transverse):
    depth = jnp.arange(layers, dtype=jnp.float32) / (layers - 1)
    helix = math.pi / 3.0 * (1.0 - 2.0 * depth)
    tilted = 0.35 * jnp.cos(math.pi * depth)
    fiber_x = jnp.cos(tilted) * jnp.cos(helix)
    fiber_y = jnp.cos(tilted) * jnp.sin(helix)
    fiber_z = jnp.sin(tilted)
    spread = longitudinal - transverse
    s_xx = transverse + spread * fiber_x * fiber_x
    s_yy = transverse + spread * fiber_y * fiber_y
    s_zz = transverse + spread * fiber_z * fiber_z
    s_xy = spread * fiber_x * fiber_y
    s_xz = spread * fiber_x * fiber_z
    s_yz = spread * fiber_y * fiber_z
    columns = [
        s_xx - jnp.abs(s_xy) - jnp.abs(s_xz),
        s_yy - jnp.abs(s_xy) - jnp.abs(s_yz),
        s_zz - jnp.abs(s_xz) - jnp.abs(s_yz),
        jnp.maximum(s_xy, 0.0),
        jnp.maximum(-s_xy, 0.0),
        jnp.maximum(s_xz, 0.0),
        jnp.maximum(-s_xz, 0.0),
        jnp.maximum(s_yz, 0.0),
        jnp.maximum(-s_yz, 0.0),
    ]
    return jnp.stack(columns, axis=1)


def window(array, offset, extent):
    return array[
        1 + offset[0] : 1 + offset[0] + extent[0],
        1 + offset[1] : 1 + offset[1] + extent[1],
        1 + offset[2] : 1 + offset[2] + extent[2],
    ]


def cell_weight(planes, column, tissue_pad, bath_pad):
    weight = tissue_pad * planes[:, column][:, None, None]
    if bath_pad is not None and column < 3:
        weight = weight + bath_sigma * bath_pad
    return weight


def edge_pair(weight, medium_pad, offset, extent):
    backward = (-offset[0], -offset[1], -offset[2])
    centre = window(medium_pad, (0, 0, 0), extent)
    own_weight = window(weight, (0, 0, 0), extent)
    forward_edge = (
        centre
        * window(medium_pad, offset, extent)
        * (0.5 * (own_weight + window(weight, offset, extent)))
    )
    backward_edge = (
        centre
        * window(medium_pad, backward, extent)
        * (0.5 * (own_weight + window(weight, backward, extent)))
    )
    return (forward_edge, backward_edge)


def with_rim(field):
    return padded(field, (("gx", 1), ("gy", 2), ("gz", 0)), 1)


def operate(field, edge_list):
    extent = field.shape
    field_pad = with_rim(field)
    summed = jnp.zeros(extent, jnp.float32)
    for column, offset in enumerate(OFFSETS):
        backward = (-offset[0], -offset[1], -offset[2])
        forward_edge, backward_edge = edge_list[column]
        summed = (
            summed
            + forward_edge * (field - window(field_pad, offset, extent))
            + backward_edge * (field - window(field_pad, backward, extent))
        )
    return summed


def body(potential, tissue_mask, layer_index, source):
    extent = tissue_mask.shape
    mask_pad = padded(tissue_mask, (("gx", 1), ("gy", 2), ("gz", 0)), 1)
    layer_pad = padded(layer_index, (("gz", 0),), 1)
    selector = (layer_pad[:, None] == jnp.arange(LAYERS, dtype=jnp.int32)[None, :]).astype(
        jnp.float32
    )
    bulk_planes = jnp.dot(
        selector, tensor_table(LAYERS, bulk_long, bulk_trans), precision=lax.Precision.HIGHEST
    )
    intra_planes = jnp.dot(
        selector, tensor_table(LAYERS, intra_long, intra_trans), precision=lax.Precision.HIGHEST
    )
    tissue_pad = (mask_pad == 2).astype(jnp.float32)
    bath_pad = (mask_pad == 1).astype(jnp.float32)
    inside_pad = (mask_pad > 0).astype(jnp.float32)
    inside = window(inside_pad, (0, 0, 0), extent)
    bulk_edges = [
        edge_pair(
            cell_weight(bulk_planes, column, tissue_pad, bath_pad), inside_pad, offset, extent
        )
        for column, offset in enumerate(OFFSETS)
    ]
    intra_edges = [
        edge_pair(cell_weight(intra_planes, column, tissue_pad, None), tissue_pad, offset, extent)
        for column, offset in enumerate(OFFSETS)
    ]
    diagonal = jnp.zeros(extent, jnp.float32)
    for forward_edge, backward_edge in bulk_edges:
        diagonal = diagonal + forward_edge + backward_edge
    jacobi = inside / jnp.maximum(diagonal, 1.0)
    rhs = -operate(potential, intra_edges) + inside * source
    count, rhs_total = lax.psum((jnp.sum(inside), jnp.sum(rhs)), ("gx", "gy", "gz"))
    residual = rhs - inside * (rhs_total / count)
    solution = jnp.zeros(extent, jnp.float32)

    def coupled(current):
        scaled = jacobi * current
        image = operate(scaled, bulk_edges)
        scaled_total, cross_total, current_total, energy_total, image_total = lax.psum(
            (
                jnp.sum(scaled),
                jnp.sum(current * scaled),
                jnp.sum(current),
                jnp.sum(scaled * image),
                jnp.sum(image),
            ),
            ("gx", "gy", "gz"),
        )
        mean_value = scaled_total / count
        precond = scaled - inside * mean_value
        gamma_value = cross_total - mean_value * current_total
        delta_value = energy_total - mean_value * image_total
        return (precond, image, gamma_value, delta_value)

    precond, image, gamma_now, delta_now = coupled(residual)
    alpha = gamma_now / delta_now
    beta_value = jnp.zeros((), jnp.float32)
    direction = jnp.zeros(extent, jnp.float32)
    along = jnp.zeros(extent, jnp.float32)
    for step in range(ITERS):
        direction = precond + beta_value * direction
        along = image + beta_value * along
        solution = solution + alpha * direction
        residual = residual - alpha * along
        if step + 1 < ITERS:
            precond, image, gamma_next, delta_now = coupled(residual)
            beta_value = gamma_next / gamma_now
            alpha = gamma_next / (delta_now - beta_value * gamma_next / alpha)
            gamma_now = gamma_next
    return (solution, residual)


def solution(mesh):
    placed = (P("gz", "gx", "gy"), P("gz", "gx", "gy"), P("gz"), P("gz", "gx", "gy"))
    return jax.shard_map(
        body,
        mesh=mesh,
        in_specs=placed,
        out_specs=(P("gz", "gx", "gy"), P("gz", "gx", "gy")),
        check_vma=False,
    )
```

profile of v0, /device:TPU:0, one launch (start us, length us, event | category | flops | bytes accessed | tf_op | source)
XLA Modules:
  0.0 655.7 jit_solution(4429758000166814855)
XLA Ops:
  0.6 1.3 fusion.493
  1.9 3.0 collective-permute-start.6
  7.0 4.3 collective-permute-start
  13.4 4.5 collective-permute-start.9
  20.3 1.3 pad_add_fusion.7
  22.1 2.4 collective-permute-done.8
  24.6 3.4 collective-permute-start.11
  29.5 4.6 collective-permute-start.2
  38.1 4.1 collective-permute-done.3
  45.1 1.6 collective-permute-done.5
  47.2 1.7 broadcast_select_fusion
  50.7 1.9 fusion.471
  52.6 40.0 %all-reduce.8 = (f32[]{:T(128)}, f32[]{:T(128)}) all-reduce(f32[]{:T(128)} %get-tuple-element.130, f32[]{:T(128)} %slice_reduce_fusion), channel_id=1, replica_groups=mesh['gx'=4,'gy'=4,'gz'=2] {'gx','gy','gz'}, use_global_device_ids=true, to_apply=%region_1.0 | all-reduce | flops 2 | bytes 16 | tf_op jit(solution)/shard_map/psum | solution.py:154
  93.9 3.3 fusion.452
  97.3 2.2 collective-permute-start.15
  100.9 4.2 collective-permute-done.14
  105.2 4.2 collective-permute-start.17
  111.9 4.4 collective-permute-done.16
  119.1 1.6 collective-permute-done.18
  122.2 40.4 %all-reduce.7 = (f32[]{:T(128)}, f32[]{:T(128)}, f32[]{:T(128)}, f32[]{:T(128)}, f32[]{:T(128)}) all-reduce(f32[]{:T(128)} %get-tuple-element.40, f32[]{:T(128)} %get-tuple-element.39, f32[]{:T(128)} %get-tuple-element.41, f32[]{:T(128)} %get-tuple-element.38, ...), channel_id=1, replica_groups=mesh['gx'=4,'gy'=4,'gz'=2] {'gx','gy','gz'}, use_global_device_ids=true, to_apply=%region_5.0 | all-reduce | flops 5 | bytes 40 | tf_op jit(solution)/shard_map/psum | solution.py:161
  166.6 2.2 collective-permute-start.21
  170.1 4.2 collective-permute-done.20
  174.4 4.2 collective-permute-start.23
  181.1 4.4 collective-permute-done.22
  188.4 1.6 collective-permute-done.24
  191.5 40.5 %all-reduce.6 = (f32[]{:T(128)}, f32[]{:T(128)}, f32[]{:T(128)}, f32[]{:T(128)}, f32[]{:T(128)}) all-reduce(f32[]{:T(128)} %get-tuple-element.35, f32[]{:T(128)} %get-tuple-element.34, f32[]{:T(128)} %get-tuple-element.36, f32[]{:T(128)} %get-tuple-element.33, ...), channel_id=1, replica_groups=mesh['gx'=4,'gy'=4,'gz'=2] {'gx','gy','gz'}, use_global_device_ids=true, to_apply=%region_15.0 | all-reduce | flops 5 | bytes 40 | tf_op jit(solution)/shard_map/psum | solution.py:161
  236.0 2.2 collective-permute-start.27
  239.5 4.2 collective-permute-done.26
  243.8 4.2 collective-permute-start.29
  248.0 1.5 collective-permute-start.28
  250.5 4.4 collective-permute-done.28
  257.7 1.6 collective-permute-done.30
  260.8 40.6 %all-reduce.5 = (f32[]{:T(128)}, f32[]{:T(128)}, f32[]{:T(128)}, f32[]{:T(128)}, f32[]{:T(128)}) all-reduce(f32[]{:T(128)} %get-tuple-element.30, f32[]{:T(128)} %get-tuple-element.29, f32[]{:T(128)} %get-tuple-element.31, f32[]{:T(128)} %get-tuple-element.28, ...), channel_id=1, replica_groups=mesh['gx'=4,'gy'=4,'gz'=2] {'gx','gy','gz'}, use_global_device_ids=true, to_apply=%region_25.0 | all-reduce | flops 5 | bytes 40 | tf_op jit(solution)/shard_map/psum | solution.py:161
  305.4 2.1 collective-permute-start.33
  308.9 4.2 collective-permute-done.32
  313.2 4.2 collective-permute-start.35
  319.9 4.4 collective-permute-done.34
  327.1 1.6 collective-permute-done.36
  330.2 40.6 %all-reduce.4 = (f32[]{:T(128)}, f32[]{:T(128)}, f32[]{:T(128)}, f32[]{:T(128)}, f32[]{:T(128)}) all-reduce(f32[]{:T(128)} %get-tuple-element.25, f32[]{:T(128)} %get-tuple-element.24, f32[]{:T(128)} %get-tuple-element.26, f32[]{:T(128)} %get-tuple-element.23, ...), channel_id=1, replica_groups=mesh['gx'=4,'gy'=4,'gz'=2] {'gx','gy','gz'}, use_global_device_ids=true, to_apply=%region_35.0 | all-reduce | flops 5 | bytes 40 | tf_op jit(solution)/shard_map/psum | solution.py:161
  374.9 2.1 collective-permute-start.39
  378.2 4.2 collective-permute-done.38
  382.6 4.2 collective-permute-start.41
  389.3 4.4 collective-permute-done.40
  396.5 1.6 collective-permute-done.42
  399.6 40.7 %all-reduce.3 = (f32[]{:T(128)}, f32[]{:T(128)}, f32[]{:T(128)}, f32[]{:T(128)}, f32[]{:T(128)}) all-reduce(f32[]{:T(128)} %get-tuple-element.20, f32[]{:T(128)} %get-tuple-element.19, f32[]{:T(128)} %get-tuple-element.21, f32[]{:T(128)} %get-tuple-element.18, ...), channel_id=1, replica_groups=mesh['gx'=4,'gy'=4,'gz'=2] {'gx','gy','gz'}, use_global_device_ids=true, to_apply=%region_45.0 | all-reduce | flops 5 | bytes 40 | tf_op jit(solution)/shard_map/psum | solution.py:161
  444.3 2.0 collective-permute-start.45
  447.6 4.2 collective-permute-done.44
  452.0 4.2 collective-permute-start.47
  458.6 4.4 collective-permute-done.46
  465.9 1.6 collective-permute-done.48
  469.0 40.7 %all-reduce.2 = (f32[]{:T(128)}, f32[]{:T(128)}, f32[]{:T(128)}, f32[]{:T(128)}, f32[]{:T(128)}) all-reduce(f32[]{:T(128)} %get-tuple-element.15, f32[]{:T(128)} %get-tuple-element.14, f32[]{:T(128)} %get-tuple-element.16, f32[]{:T(128)} %get-tuple-element.13, ...), channel_id=1, replica_groups=mesh['gx'=4,'gy'=4,'gz'=2] {'gx','gy','gz'}, use_global_device_ids=true, to_apply=%region_55.0 | all-reduce | flops 5 | bytes 40 | tf_op jit(solution)/shard_map/psum | solution.py:161
  513.7 2.0 collective-permute-start.51
  517.1 4.2 collective-permute-done.50
  521.4 4.2 collective-permute-start.53
  528.1 4.4 collective-permute-done.52
  535.3 1.6 collective-permute-done.54
  537.3 1.8 fusion.430
  539.1 40.7 %all-reduce.1 = (f32[]{:T(128)}, f32[]{:T(128)}, f32[]{:T(128)}, f32[]{:T(128)}, f32[]{:T(128)}) all-reduce(f32[]{:T(128)} %get-tuple-element.10, f32[]{:T(128)} %get-tuple-element.9, f32[]{:T(128)} %get-tuple-element.11, f32[]{:T(128)} %get-tuple-element.8, f32[]{:T(128)} %get-tuple-element.7), channel_id=1, replica_groups=mesh['gx'=4,'gy'=4,'gz'=2] {'gx','gy','gz'}, use_global_device_ids=true, to_apply=%region_65.0 | all-reduce | flops 5 | bytes 40 | tf_op jit(solution)/shard_map/psum | solution.py:161
  584.7 2.0 collective-permute-start.57
  588.1 4.2 collective-permute-done.56
  592.4 4.2 collective-permute-start.59
  599.1 4.4 collective-permute-done.58
  606.4 1.6 collective-permute-done.60
  609.5 40.7 %all-reduce = (f32[]{:T(128)}, f32[]{:T(128)}, f32[]{:T(128)}, f32[]{:T(128)}, f32[]{:T(128)}) all-reduce(f32[]{:T(128)} %get-tuple-element.5, f32[]{:T(128)} %get-tuple-element.4, f32[]{:T(128)} %get-tuple-element.6, f32[]{:T(128)} %get-tuple-element.3, f32[]{:T(128)} %get-tuple-element.2), channel_id=1, replica_groups=mesh['gx'=4,'gy'=4,'gz'=2] {'gx','gy','gz'}, use_global_device_ids=true, to_apply=%region_75.0 | all-reduce | flops 5 | bytes 40 | tf_op jit(solution)/shard_map/psum | solution.py:161
  (178 shorter events, 83.5 us)
Async XLA Ops:
  1.9 17.1 %collective-permute-start.6 = (s32[1]{0:T(128)}, s32[1]{0:T(128)}, u32[]{:S(2)}, u32[]{:S(2)}) collective-permute-start(s32[1]{0:T(128)} %get-tuple-element.268), channel_id=1, source_target_pairs={{0,1},{2,3},{4,5},{6,7},{8,9},{10,11},{12,13},{14,15},{16,17},{18,... | collective-permute-start | bytes 20 | tf_op jit(solution)/shard_map/ppermute | solution.py:37
  4.9 15.4 %collective-permute-start.7 = (s32[1]{0:T(128)}, s32[1]{0:T(128)}, u32[]{:S(2)}, u32[]{:S(2)}) collective-permute-start(s32[1]{0:T(128)} %get-tuple-element.269), channel_id=1, source_target_pairs={{1,0},{3,2},{5,4},{7,6},{9,8},{11,10},{13,12},{15,14},{17,16},{19,... | collective-permute-start | bytes 20 | tf_op jit(solution)/shard_map/ppermute | solution.py:38
  7.0 22.4 %collective-permute-start = (s32[8,1,128]{2,1,0:T(1,128)S(1)}, s32[8,1,128]{2,1,0:T(1,128)S(1)}, u32[]{:S(2)}, u32[]{:S(2)}) collective-permute-start(s32[8,1,128]{2,1,0:T(1,128)S(1)} %get-tuple-element.232), channel_id=1, source_target_pairs={{0,8},{8,16},{16,24},{1,9},{9,17},{17,25},{2,10},{10,18},{18,26},{... | collective-permute-start | bytes 12296 | tf_op jit(solution)/shard_map/ppermute | solution.py:37
  11.3 18.1 %collective-permute-start.1 = (s32[8,1,128]{2,1,0:T(1,128)S(1)}, s32[8,1,128]{2,1,0:T(1,128)S(1)}, u32[]{:S(2)}, u32[]{:S(2)}) collective-permute-start(s32[8,1,128]{2,1,0:T(1,128)S(1)} %get-tuple-element.233), channel_id=1, source_target_pairs={{8,0},{16,8},{24,16},{9,1},{17,9},{25,17},{10,2},{18,10},{26,18},{... | collective-permute-start | bytes 12296 | tf_op jit(solution)/shard_map/ppermute | solution.py:38
  13.4 8.7 %collective-permute-start.9 = (f32[8,1,128]{2,1,0:T(1,128)S(1)}, f32[8,1,128]{2,1,0:T(1,128)S(1)}, u32[]{:S(2)}, u32[]{:S(2)}) collective-permute-start(f32[8,1,128]{2,1,0:T(1,128)S(1)} %get-tuple-element.230), channel_id=1, source_target_pairs={{0,8},{8,16},{16,24},{1,9},{9,17},{17,25},{2,10},{10,18},{18,26},{... | collective-permute-start | bytes 12296 | tf_op jit(solution)/shard_map/ppermute | solution.py:37
  18.9 5.6 copy-start.1
  19.0 5.5 collective-permute-start.8
  24.5 4.8 copy-start
  24.6 10.7 %collective-permute-start.11 = (f32[8,26,1]{2,1,0:T(8,128)S(1)}, f32[8,26,1]{2,1,0:T(8,128)S(1)}, u32[]{:S(2)}, u32[]{:S(2)}) collective-permute-start(f32[8,26,1]{2,1,0:T(8,128)S(1)} %get-tuple-element.192), channel_id=1, source_target_pairs={{0,2},{2,4},{4,6},{1,3},{3,5},{5,7},{8,10},{10,12},{12,14},{9,11},... | collective-permute-start | bytes 2504 | tf_op jit(solution)/shard_map/ppermute | solution.py:37
  28.1 7.3 %collective-permute-start.10 = (f32[8,26,1]{2,1,0:T(8,128)S(1)}, f32[8,26,1]{2,1,0:T(8,128)S(1)}, u32[]{:S(2)}, u32[]{:S(2)}) collective-permute-start(f32[8,26,1]{2,1,0:T(8,128)S(1)} %get-tuple-element.193), channel_id=1, source_target_pairs={{2,0},{4,2},{6,4},{3,1},{5,3},{7,5},{10,8},{12,10},{14,12},{11,9},... | collective-permute-start | bytes 2504 | tf_op jit(solution)/shard_map/ppermute | solution.py:38
  29.5 8.6 %collective-permute-start.2 = (s32[8,26,1]{2,1,0:T(8,128)S(1)}, s32[8,26,1]{2,1,0:T(8,128)S(1)}, u32[]{:S(2)}, u32[]{:S(2)}) collective-permute-start(s32[8,26,1]{2,1,0:T(8,128)S(1)} %get-tuple-element.194), channel_id=1, source_target_pairs={{0,2},{2,4},{4,6},{1,3},{3,5},{5,7},{8,10},{10,12},{12,14},{9,11},... | collective-permute-start | bytes 2504 | tf_op jit(solution)/shard_map/ppermute | solution.py:37
  34.1 8.1 %collective-permute-start.3 = (s32[8,26,1]{2,1,0:T(8,128)S(1)}, s32[8,26,1]{2,1,0:T(8,128)S(1)}, u32[]{:S(2)}, u32[]{:S(2)}) collective-permute-start(s32[8,26,1]{2,1,0:T(8,128)S(1)} %get-tuple-element.195), channel_id=1, source_target_pairs={{2,0},{4,2},{6,4},{3,1},{5,3},{7,5},{10,8},{12,10},{14,12},{11,9},... | collective-permute-start | bytes 2504 | tf_op jit(solution)/shard_map/ppermute | solution.py:38
  35.5 14.3 %collective-permute-start.13 = (f32[1,26,130]{2,1,0:T(8,128)S(1)}, f32[1,26,130]{2,1,0:T(8,128)S(1)}, u32[]{:S(2)}, u32[]{:S(2)}) collective-permute-start(f32[1,26,130]{2,1,0:T(8,128)S(1)} %get-tuple-element.170), channel_id=1, source_target_pairs={{0,1},{2,3},{4,5},{6,7},{8,9},{10,11},{12,13},{14,15},{16,17},{18,... | collective-permute-start | bytes 40568 | tf_op jit(solution)/shard_map/ppermute | solution.py:37
  36.8 13.0 %collective-permute-start.12 = (f32[1,26,130]{2,1,0:T(8,128)S(1)}, f32[1,26,130]{2,1,0:T(8,128)S(1)}, u32[]{:S(2)}, u32[]{:S(2)}) collective-permute-start(f32[1,26,130]{2,1,0:T(8,128)S(1)} %get-tuple-element.171), channel_id=1, source_target_pairs={{1,0},{3,2},{5,4},{7,6},{9,8},{11,10},{13,12},{15,14},{17,16},{19,... | collective-permute-start | bytes 40568 | tf_op jit(solution)/shard_map/ppermute | solution.py:38
  42.3 2.8 collective-permute-start.4
  43.6 3.1 collective-permute-start.5
  97.3 3.6 collective-permute-start.15
  99.6 5.5 collective-permute-start.14
  105.2 6.7 %collective-permute-start.17 = (f32[8,26,1]{2,1,0:T(8,128)S(1)}, f32[8,26,1]{2,1,0:T(8,128)S(1)}, u32[]{:S(2)}, u32[]{:S(2)}) collective-permute-start(f32[8,26,1]{2,1,0:T(8,128)S(1)} %get-tuple-element.190), channel_id=1, source_target_pairs={{0,2},{2,4},{4,6},{1,3},{3,5},{5,7},{8,10},{10,12},{12,14},{9,11},... | collective-permute-start | bytes 2504 | tf_op jit(solution)/shard_map/ppermute | solution.py:37
  109.4 6.9 %collective-permute-start.16 = (f32[8,26,1]{2,1,0:T(8,128)S(1)}, f32[8,26,1]{2,1,0:T(8,128)S(1)}, u32[]{:S(2)}, u32[]{:S(2)}) collective-permute-start(f32[8,26,1]{2,1,0:T(8,128)S(1)} %get-tuple-element.191), channel_id=1, source_target_pairs={{2,0},{4,2},{6,4},{3,1},{5,3},{7,5},{10,8},{12,10},{14,12},{11,9},... | collective-permute-start | bytes 2504 | tf_op jit(solution)/shard_map/ppermute | solution.py:38
  116.3 2.8 collective-permute-start.19
  117.6 3.1 collective-permute-start.18
  166.6 3.5 collective-permute-start.21
  168.8 5.5 collective-permute-start.20
  174.4 6.7 %collective-permute-start.23 = (f32[8,26,1]{2,1,0:T(8,128)S(1)}, f32[8,26,1]{2,1,0:T(8,128)S(1)}, u32[]{:S(2)}, u32[]{:S(2)}) collective-permute-start(f32[8,26,1]{2,1,0:T(8,128)S(1)} %get-tuple-element.188), channel_id=1, source_target_pairs={{0,2},{2,4},{4,6},{1,3},{3,5},{5,7},{8,10},{10,12},{12,14},{9,11},... | collective-permute-start | bytes 2504 | tf_op jit(solution)/shard_map/ppermute | solution.py:37
  178.6 6.9 %collective-permute-start.22 = (f32[8,26,1]{2,1,0:T(8,128)S(1)}, f32[8,26,1]{2,1,0:T(8,128)S(1)}, u32[]{:S(2)}, u32[]{:S(2)}) collective-permute-start(f32[8,26,1]{2,1,0:T(8,128)S(1)} %get-tuple-element.189), channel_id=1, source_target_pairs={{2,0},{4,2},{6,4},{3,1},{5,3},{7,5},{10,8},{12,10},{14,12},{11,9},... | collective-permute-start | bytes 2504 | tf_op jit(solution)/shard_map/ppermute | solution.py:38
  185.6 2.8 collective-permute-start.25
  186.9 3.1 collective-permute-start.24
  236.0 3.5 collective-permute-start.27
  238.2 5.5 collective-permute-start.26
  243.8 6.7 %collective-permute-start.29 = (f32[8,26,1]{2,1,0:T(8,128)S(1)}, f32[8,26,1]{2,1,0:T(8,128)S(1)}, u32[]{:S(2)}, u32[]{:S(2)}) collective-permute-start(f32[8,26,1]{2,1,0:T(8,128)S(1)} %get-tuple-element.186), channel_id=1, source_target_pairs={{0,2},{2,4},{4,6},{1,3},{3,5},{5,7},{8,10},{10,12},{12,14},{9,11},... | collective-permute-start | bytes 2504 | tf_op jit(solution)/shard_map/ppermute | solution.py:37
  248.0 6.9 %collective-permute-start.28 = (f32[8,26,1]{2,1,0:T(8,128)S(1)}, f32[8,26,1]{2,1,0:T(8,128)S(1)}, u32[]{:S(2)}, u32[]{:S(2)}) collective-permute-start(f32[8,26,1]{2,1,0:T(8,128)S(1)} %get-tuple-element.187), channel_id=1, source_target_pairs={{2,0},{4,2},{6,4},{3,1},{5,3},{7,5},{10,8},{12,10},{14,12},{11,9},... | collective-permute-start | bytes 2504 | tf_op jit(solution)/shard_map/ppermute | solution.py:38
  255.0 2.8 collective-permute-start.31
  256.3 3.1 collective-permute-start.30
  305.4 3.4 collective-permute-start.33
  307.6 5.5 collective-permute-start.32
  313.2 6.7 %collective-permute-start.35 = (f32[8,26,1]{2,1,0:T(8,128)S(1)}, f32[8,26,1]{2,1,0:T(8,128)S(1)}, u32[]{:S(2)}, u32[]{:S(2)}) collective-permute-start(f32[8,26,1]{2,1,0:T(8,128)S(1)} %get-tuple-element.184), channel_id=1, source_target_pairs={{0,2},{2,4},{4,6},{1,3},{3,5},{5,7},{8,10},{10,12},{12,14},{9,11},... | collective-permute-start | bytes 2504 | tf_op jit(solution)/shard_map/ppermute | solution.py:37
  317.4 6.9 %collective-permute-start.34 = (f32[8,26,1]{2,1,0:T(8,128)S(1)}, f32[8,26,1]{2,1,0:T(8,128)S(1)}, u32[]{:S(2)}, u32[]{:S(2)}) collective-permute-start(f32[8,26,1]{2,1,0:T(8,128)S(1)} %get-tuple-element.185), channel_id=1, source_target_pairs={{2,0},{4,2},{6,4},{3,1},{5,3},{7,5},{10,8},{12,10},{14,12},{11,9},... | collective-permute-start | bytes 2504 | tf_op jit(solution)/shard_map/ppermute | solution.py:38
  324.3 2.8 collective-permute-start.37
  325.6 3.1 collective-permute-start.36
  374.9 3.4 collective-permute-start.39
  376.9 5.5 collective-permute-start.38
  382.6 6.7 %collective-permute-start.41 = (f32[8,26,1]{2,1,0:T(8,128)S(1)}, f32[8,26,1]{2,1,0:T(8,128)S(1)}, u32[]{:S(2)}, u32[]{:S(2)}) collective-permute-start(f32[8,26,1]{2,1,0:T(8,128)S(1)} %get-tuple-element.182), channel_id=1, source_target_pairs={{0,2},{2,4},{4,6},{1,3},{3,5},{5,7},{8,10},{10,12},{12,14},{9,11},... | collective-permute-start | bytes 2504 | tf_op jit(solution)/shard_map/ppermute | solution.py:37
  386.8 6.9 %collective-permute-start.40 = (f32[8,26,1]{2,1,0:T(8,128)S(1)}, f32[8,26,1]{2,1,0:T(8,128)S(1)}, u32[]{:S(2)}, u32[]{:S(2)}) collective-permute-start(f32[8,26,1]{2,1,0:T(8,128)S(1)} %get-tuple-element.183), channel_id=1, source_target_pairs={{2,0},{4,2},{6,4},{3,1},{5,3},{7,5},{10,8},{12,10},{14,12},{11,9},... | collective-permute-start | bytes 2504 | tf_op jit(solution)/shard_map/ppermute | solution.py:38
  393.7 2.8 collective-permute-start.43
  395.0 3.1 collective-permute-start.42
  444.3 3.4 collective-permute-start.45
  446.3 5.5 collective-permute-start.44
  452.0 6.7 %collective-permute-start.47 = (f32[8,26,1]{2,1,0:T(8,128)S(1)}, f32[8,26,1]{2,1,0:T(8,128)S(1)}, u32[]{:S(2)}, u32[]{:S(2)}) collective-permute-start(f32[8,26,1]{2,1,0:T(8,128)S(1)} %get-tuple-element.180), channel_id=1, source_target_pairs={{0,2},{2,4},{4,6},{1,3},{3,5},{5,7},{8,10},{10,12},{12,14},{9,11},... | collective-permute-start | bytes 2504 | tf_op jit(solution)/shard_map/ppermute | solution.py:37
  456.2 6.9 %collective-permute-start.46 = (f32[8,26,1]{2,1,0:T(8,128)S(1)}, f32[8,26,1]{2,1,0:T(8,128)S(1)}, u32[]{:S(2)}, u32[]{:S(2)}) collective-permute-start(f32[8,26,1]{2,1,0:T(8,128)S(1)} %get-tuple-element.181), channel_id=1, source_target_pairs={{2,0},{4,2},{6,4},{3,1},{5,3},{7,5},{10,8},{12,10},{14,12},{11,9},... | collective-permute-start | bytes 2504 | tf_op jit(solution)/shard_map/ppermute | solution.py:38
  463.1 2.8 collective-permute-start.49
  464.4 3.1 collective-permute-start.48
  513.7 3.4 collective-permute-start.51
  515.8 5.5 collective-permute-start.50
  521.4 6.7 %collective-permute-start.53 = (f32[8,26,1]{2,1,0:T(8,128)S(1)}, f32[8,26,1]{2,1,0:T(8,128)S(1)}, u32[]{:S(2)}, u32[]{:S(2)}) collective-permute-start(f32[8,26,1]{2,1,0:T(8,128)S(1)} %get-tuple-element.178), channel_id=1, source_target_pairs={{0,2},{2,4},{4,6},{1,3},{3,5},{5,7},{8,10},{10,12},{12,14},{9,11},... | collective-permute-start | bytes 2504 | tf_op jit(solution)/shard_map/ppermute | solution.py:37
  525.6 6.9 %collective-permute-start.52 = (f32[8,26,1]{2,1,0:T(8,128)S(1)}, f32[8,26,1]{2,1,0:T(8,128)S(1)}, u32[]{:S(2)}, u32[]{:S(2)}) collective-permute-start(f32[8,26,1]{2,1,0:T(8,128)S(1)} %get-tuple-element.179), channel_id=1, source_target_pairs={{2,0},{4,2},{6,4},{3,1},{5,3},{7,5},{10,8},{12,10},{14,12},{11,9},... | collective-permute-start | bytes 2504 | tf_op jit(solution)/shard_map/ppermute | solution.py:38
  532.5 2.8 collective-permute-start.55
  533.8 3.1 collective-permute-start.54
  584.7 3.4 collective-permute-start.57
  586.8 5.5 collective-permute-start.56
  592.4 6.7 %collective-permute-start.59 = (f32[8,26,1]{2,1,0:T(8,128)S(1)}, f32[8,26,1]{2,1,0:T(8,128)S(1)}, u32[]{:S(2)}, u32[]{:S(2)}) collective-permute-start(f32[8,26,1]{2,1,0:T(8,128)S(1)} %get-tuple-element.176), channel_id=1, source_target_pairs={{0,2},{2,4},{4,6},{1,3},{3,5},{5,7},{8,10},{10,12},{12,14},{9,11},... | collective-permute-start | bytes 2504 | tf_op jit(solution)/shard_map/ppermute | solution.py:37
  596.6 6.9 %collective-permute-start.58 = (f32[8,26,1]{2,1,0:T(8,128)S(1)}, f32[8,26,1]{2,1,0:T(8,128)S(1)}, u32[]{:S(2)}, u32[]{:S(2)}) collective-permute-start(f32[8,26,1]{2,1,0:T(8,128)S(1)} %get-tuple-element.177), channel_id=1, source_target_pairs={{2,0},{4,2},{6,4},{3,1},{5,3},{7,5},{10,8},{12,10},{14,12},{11,9},... | collective-permute-start | bytes 2504 | tf_op jit(solution)/shard_map/ppermute | solution.py:38
  603.6 2.8 collective-permute-start.61
  604.9 3.1 collective-permute-start.60
  (2 other events, 2.3 us)
where the time goes:
time: 659 us; the launch traced here: 656 us
  blocking collectives  365 us (55%)
  starting transfers between devices  123 us (19%)
  waiting for transfers between devices  99 us (15%)
  between operations  34.8 us (5%)
  other arithmetic  28.8 us (4%)
    psum x8, blocking collectives, coupled(): lax.psum((jnp.sum(scaled), jnp.sum(current * scaled), jnp.sum(current), j...  325 us
    ppermute x31, waiting for transfers between devices, padded(): after = lax.ppermute(first, axis, down)  89.5 us
    ppermute x31, starting transfers between devices, padded(): before = lax.ppermute(last, axis, up)  83 us
    ppermute x31, starting transfers between devices, padded(): after = lax.ppermute(first, axis, down)  40.2 us
    psum x1, blocking collectives, body(): lax.psum((jnp.sum(inside), jnp.sum(rhs)), ('gx', 'gy', 'gz'))  40 us
  transfers between devices with their start and end apart: 62, of which 35 were waited for; matrix products, arithmetic and copies ran while one was open for 1% of the time, Pallas kernels for 0%

commit v1 on v0

v1 whole, which is shorter than its diff:
```python
import functools
import math

import jax
import jax.numpy as jnp
from jax import lax
from jax.experimental import pallas as pl
from jax.experimental.pallas import tpu as pltpu
from jax.sharding import PartitionSpec as P

ITERS = 8
DEPTH = ITERS + 1
LAYERS = 16
AXES = ("gx", "gy", "gz")

OFFSETS = [
    (0, 1, 0),
    (0, 0, 1),
    (1, 0, 0),
    (0, 1, 1),
    (0, 1, -1),
    (1, 1, 0),
    (-1, 1, 0),
    (1, 0, 1),
    (-1, 0, 1),
]
bulk_long = 7.99
bulk_trans = 2.55
intra_long = 1.74
intra_trans = 0.19
bath_sigma = 5.0


def tensor_table(layers, longitudinal, transverse):
    depth = jnp.arange(layers, dtype=jnp.float32) / (layers - 1)
    helix = math.pi / 3.0 * (1.0 - 2.0 * depth)
    tilted = 0.35 * jnp.cos(math.pi * depth)
    fiber_x = jnp.cos(tilted) * jnp.cos(helix)
    fiber_y = jnp.cos(tilted) * jnp.sin(helix)
    fiber_z = jnp.sin(tilted)
    spread = longitudinal - transverse
    s_xx = transverse + spread * fiber_x * fiber_x
    s_yy = transverse + spread * fiber_y * fiber_y
    s_zz = transverse + spread * fiber_z * fiber_z
    s_xy = spread * fiber_x * fiber_y
    s_xz = spread * fiber_x * fiber_z
    s_yz = spread * fiber_y * fiber_z
    columns = [
        s_xx - jnp.abs(s_xy) - jnp.abs(s_xz),
        s_yy - jnp.abs(s_xy) - jnp.abs(s_yz),
        s_zz - jnp.abs(s_xz) - jnp.abs(s_yz),
        jnp.maximum(s_xy, 0.0),
        jnp.maximum(-s_xy, 0.0),
        jnp.maximum(s_xz, 0.0),
        jnp.maximum(-s_xz, 0.0),
        jnp.maximum(s_yz, 0.0),
        jnp.maximum(-s_yz, 0.0),
    ]
    return jnp.stack(columns, axis=1)


def shifted(value, axis, hop):
    count = lax.axis_size(axis)
    pairs = [(i + hop, i) for i in range(count) if 0 <= i + hop < count]
    return lax.ppermute(value, axis, pairs)


def framed(value, axis, dim, multiple):
    count, length = lax.axis_size(axis), value.shape[dim]
    if count == 1:
        return value
    if count == 2 and 2 * length <= length + 2 * DEPTH and multiple == 1:
        other = lax.ppermute(value, axis, [(0, 1), (1, 0)])
        return jnp.concatenate([value, other], axis=dim)
    after, before = [], []
    left, hop = DEPTH, 1
    while left > 0:
        width = min(left, length)
        if hop < count:
            after.append(
                shifted(lax.slice_in_dim(value, 0, width, axis=dim), axis, hop)
            )
            before.insert(
                0, shifted(lax.slice_in_dim(value, length - width, length, axis=dim), axis, -hop)
            )
        else:
            shape = list(value.shape)
            shape[dim] = width
            after.append(jnp.zeros(shape, value.dtype))
            before.insert(0, jnp.zeros(shape, value.dtype))
        left, hop = left - width, hop + 1
    gap = -(length + 2 * DEPTH) % multiple
    shape = list(value.shape)
    shape[dim] = gap
    middle = [jnp.zeros(shape, value.dtype)] if gap else []
    return jnp.concatenate([value] + after + middle + before, axis=dim)


def fields_around(ref, here, above, below, rows, lanes):
    def along_x(value, step):
        return pltpu.roll(value, (-step) % rows, 0)

    def along_y(value, step):
        return pltpu.roll(value, (-step) % lanes, 1)

    for dz, plane in ((0, here), (1, above), (-1, below)):
        value = ref[plane]
        if dz:
            yield (dz, 0, 0), value
        for step in (1, -1):
            yield (dz, step, 0), along_x(value, step)
        for step in (1, -1):
            moved = along_y(value, step)
            yield (dz, 0, step), moved
            if dz == 0:
                for other in (1, -1):
                    yield (0, other, step), along_x(moved, other)


SLOT = {}
for _column, _offset in enumerate(OFFSETS):
    SLOT[_offset] = (_column, 2 * _column)
    SLOT[tuple(-o for o in _offset)] = (_column, 2 * _column + 1)


def powers_kernel(extent, table, stats, mask, potential, source, basis, scale, dots,
                  weights, spare, first, second, jac):
    planes, rows, lanes = mask.shape
    nz, nx, ny = extent
    mean_rhs = stats[0]

    def neighbours(plane):
        above = jnp.where(plane + 1 == planes, 0, plane + 1)
        below = jnp.where(plane == 0, planes - 1, plane - 1)
        return above, below

    def setup(plane, carry):
        above, below = neighbours(plane)
        labels = mask[plane]
        tissue = jnp.where(labels == 2.0, 1.0, 0.0)
        bath = jnp.where(labels == 1.0, 1.0, 0.0)
        inside = tissue + bath
        volts = potential[plane]
        total = jnp.zeros((rows, lanes), jnp.float32)
        image = jnp.zeros((rows, lanes), jnp.float32)
        pairs = zip(
            fields_around(mask, plane, above, below, rows, lanes),
            fields_around(potential, plane, above, below, rows, lanes),
        )
        for (offset, label), (_, volt) in pairs:
            column, slot = SLOT[offset]
            beyond = {0: plane, 1: above, -1: below}[offset[0]]
            link = 0.5
            if offset[0] == 1:
                link = 0.5 * table[plane, 18]
            if offset[0] == -1:
                link = 0.5 * table[below, 18]
            their_tissue = jnp.where(label == 2.0, 1.0, 0.0)
            g_here, g_there = table[plane, column] * link, table[beyond, column] * link
            weight = tissue * g_here
            if column < 3:
                their_bath = jnp.where(label == 1.0, 1.0, 0.0)
                sigma = bath_sigma * link
                weight = inside * (
                    jnp.where(label > 0.0, weight + bath * sigma, 0.0)
                    + (their_tissue * g_there + their_bath * sigma)
                )
            else:
                weight = inside * (jnp.where(label > 0.0, weight, 0.0) + their_tissue * g_there)
            weights[slot, plane] = weight
            total = total + weight
            intra = (table[plane, 9 + column] + table[beyond, 9 + column]) * link
            image = image + (tissue * their_tissue * intra) * (volts - volt)
        bounded = jnp.maximum(total, 1.0)
        jacobi = inside / bounded
        jac[plane] = jacobi + jacobi
        spare[plane] = inside * (1.0 - jacobi * total)
        first[plane] = jacobi * (inside * source[plane] - image - inside * mean_rhs)

        @pl.when(plane < nz)
        def _():
            scale[plane] = (inside * bounded)[:nx, :ny]

        return carry

    lax.fori_loop(0, planes, setup, 0)

    def record(step, now, before):
        rowsum = jnp.zeros((1, ny), jnp.float32)
        square, cross, plain = rowsum, rowsum, rowsum
        for plane in range(nz):
            value = now[plane, 0:nx, 0:ny]
            basis[step, plane] = value
            weighted = value * scale[plane]
            square = square + jnp.sum(weighted * value, axis=0, keepdims=True)
            if step:
                past = basis[step - 1, plane]
                cross = cross + jnp.sum(weighted * past, axis=0, keepdims=True)
            plain = plain + jnp.sum(value, axis=0, keepdims=True)
        if step < ITERS:
            dots[pl.ds(2 * step, 1)] = square
            dots[pl.ds(2 * ITERS + step, 1)] = plain
        if step:
            dots[pl.ds(2 * step - 1, 1)] = cross

    record(0, first, None)

    def apply(now, old, start):
        def one(plane, carry):
            above, below = neighbours(plane)
            total = jnp.zeros((rows, lanes), jnp.float32)
            for offset, value in fields_around(now, plane, above, below, rows, lanes):
                total = total + weights[SLOT[offset][1], plane] * value
            if start:
                old[plane] = 0.5 * jac[plane] * total + spare[plane] * now[plane]
            else:
                old[plane] = (
                    jac[plane] * total + 2.0 * spare[plane] * now[plane] - old[plane]
                )
            return carry

        lax.fori_loop(0, planes, one, 0)

    now, old = first, second
    for step in range(1, ITERS + 1):
        apply(now, old, step == 1)
        now, old = old, now
        record(step, now, old)


def combine_kernel(raw, count, basis, scale, phi, residual):
    nz = scale.shape[0]
    lane = lax.broadcasted_iota(jnp.int32, (1, 128), 1)
    sums = raw[...]

    def pick(vector, index):
        return jnp.sum(jnp.where(lane == index, vector, 0.0), axis=1, keepdims=True)

    def left(vector):
        return pltpu.roll(vector, 127, 1)

    def right(vector):
        return pltpu.roll(vector, 1, 1)

    mu0, mu1 = pick(sums, 0), pick(sums, 1)
    mu = jnp.where(lane < 2, sums, 2.0 * sums - jnp.where(lane % 2 == 0, mu0, mu1))
    mu = jnp.where(lane < 2 * ITERS, mu, 0.0)
    ones = pltpu.roll(sums, 128 - 2 * ITERS, 1)
    y = jnp.where(lane == 0, 1.0, 0.0)
    p = y
    m_y, m_p = mu, mu
    x = jnp.zeros((1, 128), jnp.float32)
    rz = mu0
    for step in range(ITERS):
        h_p = p - 0.5 * (left(p) + jnp.where(lane == 1, 2.0, 1.0) * right(p))
        h_p = jnp.where(lane <= ITERS, h_p, 0.0)
        before = jnp.where(lane == 0, left(m_p), right(m_p))
        m_h = m_p - 0.5 * (left(m_p) + before)
        alpha = rz / jnp.sum(jnp.where(lane < ITERS, p * m_h, 0.0), axis=1, keepdims=True)
        x = x + alpha * p
        y = y - alpha * h_p
        m_y = m_y - alpha * m_h
        if step + 1 < ITERS:
            rz_next = jnp.sum(jnp.where(lane < ITERS, y * m_y, 0.0), axis=1, keepdims=True)
            beta = rz_next / rz
            p = y + beta * p
            m_p = m_y + beta * m_p
            rz = rz_next
    mean = jnp.sum(jnp.where(lane < ITERS, x * ones, 0.0), axis=1, keepdims=True) / count[0]
    xs = [pick(x, j) for j in range(ITERS)]
    ys = [pick(y, j) for j in range(ITERS + 1)]

    def one(plane, carry):
        weight = scale[plane]
        total = jnp.where(weight > 0.0, -mean, 0.0)
        rest = ys[ITERS] * basis[ITERS, plane]
        for j in range(ITERS):
            value = basis[j, plane]
            total = total + xs[j] * value
            rest = rest + ys[j] * value
        phi[plane] = total
        residual[plane] = weight * rest
        return carry

    lax.fori_loop(0, nz, one, 0)


def body(potential, tissue_mask, layer_index, source):
    extent = tissue_mask.shape
    nz = extent[0]
    labels = tissue_mask.astype(jnp.float32)
    own_inside = (labels > 0.0).astype(jnp.float32)
    count, rhs_total = lax.psum(
        (jnp.sum(own_inside), jnp.sum(own_inside * source)), AXES
    )
    packed = jnp.stack([labels, potential, source], axis=1)
    packed = framed(packed, "gz", 0, 1)
    packed = framed(packed, "gx", 2, 8)
    packed = framed(packed, "gy", 3, 128)
    layers = framed(layer_index, "gz", 0, 1)
    planes = layers.shape[0]
    selector = (layers[:, None] == jnp.arange(LAYERS, dtype=jnp.int32)[None, :]).astype(
        jnp.float32
    )
    tables = jnp.concatenate(
        [
            tensor_table(LAYERS, bulk_long, bulk_trans),
            tensor_table(LAYERS, intra_long, intra_trans),
        ],
        axis=1,
    )
    table = jnp.dot(selector, tables, precision=lax.Precision.HIGHEST)
    size = lax.axis_size("gz")
    link = jnp.ones((planes, 1), jnp.float32)
    if planes == size * nz:
        place = (lax.axis_index("gz") * nz + jnp.arange(planes)) % planes
        link = (place + 1 < planes).astype(jnp.float32)[:, None]
    table = jnp.concatenate([table, link], axis=1)
    frame = (planes,) + packed.shape[2:]
    smem = pl.BlockSpec(memory_space=pltpu.SMEM)
    vmem = pl.BlockSpec(memory_space=pltpu.VMEM)
    basis, scale, dots = pl.pallas_call(
        functools.partial(powers_kernel, extent),
        out_shape=(
            jax.ShapeDtypeStruct((ITERS + 1,) + extent, jnp.float32),
            jax.ShapeDtypeStruct(extent, jnp.float32),
            jax.ShapeDtypeStruct((3 * ITERS, extent[2]), jnp.float32),
        ),
        in_specs=[smem, smem, vmem, vmem, vmem],
        out_specs=(vmem, vmem, vmem),
        scratch_shapes=[pltpu.VMEM((18,) + frame, jnp.float32)]
        + [pltpu.VMEM(frame, jnp.float32)] * 4,
        compiler_params=pltpu.CompilerParams(vmem_limit_bytes=60 * 1024 * 1024),
    )(table, (rhs_total / count)[None], packed[:, 0], packed[:, 1], packed[:, 2])
    sums = lax.psum(jnp.sum(dots, axis=1), AXES)
    raw = jnp.zeros((1, 128), jnp.float32).at[0, : 3 * ITERS].set(sums)
    return tuple(
        pl.pallas_call(
            combine_kernel,
            out_shape=(jax.ShapeDtypeStruct(extent, jnp.float32),) * 2,
            in_specs=[vmem, smem, vmem, vmem],
            out_specs=(vmem, vmem),
        )(raw, count[None], basis, scale)
    )


def solution(mesh):
    placed = (P("gz", "gx", "gy"), P("gz", "gx", "gy"), P("gz"), P("gz", "gx", "gy"))
    return jax.shard_map(
        body,
        mesh=mesh,
        in_specs=placed,
        out_specs=(P("gz", "gx", "gy"), P("gz", "gx", "gy")),
        check_vma=False,
    )
```

time: 659 us -> 165 us (0.25)
  blocking collectives: 365 us -> 84.3 us
  starting transfers between devices: 123 us -> 13 us
  waiting for transfers between devices: 99 us -> 9.67 us
  Pallas kernels: 0 us -> 37.3 us
  between operations: 34.8 us -> 1.98 us
  other arithmetic: 28.8 us -> 10.6 us
    psum x9 -> x2, blocking collectives: 365 us -> 84.3 us  [the longest x1 42.2 us: body(): lax.psum((jnp.sum(own_inside), jnp.sum(own_inside * source)), AXES)]
    ppermute x62 -> x6, starting transfers between devices: 123 us -> 13 us  [the longest x4 12.4 us: shifted(): return lax.ppermute(value, axis, pairs)]
    ppermute x62 -> x6, waiting for transfers between devices: 99 us -> 9.67 us  [the longest x4 9.67 us: shifted(): return lax.ppermute(value, axis, pairs)]
    pallas_call x0 -> x2, Pallas kernels: none -> 37.3 us  [the longest x1 32.7 us: body(): pl.pallas_call(functools.partial(powers_kernel, extent), out_shape=(jax.S...]
    reduce_sum x10 -> x2, other arithmetic: 12.4 us -> 2.46 us  [the longest x1 1.64 us: body(): jnp.sum(own_inside)]
  transfers between devices with their start and end apart: 62 -> 6, of which waited for: 35 -> 3; matrix products, arithmetic and copies ran while one was open for 1% -> 3% of each run, Pallas kernels for 0% -> 0%
where the time goes in v1:
time: 165 us; the launch traced here: 164 us
  blocking collectives  84.3 us (51%)
  Pallas kernels  37.3 us (23%)
  starting transfers between devices  13 us (8%)
  other arithmetic  10.6 us (6%)
  waiting for transfers between devices  9.67 us (6%)
  local copies, waits for them, and re-layouts  7.06 us (4%)
  between operations  1.98 us (1%)
    psum x1, blocking collectives, body(): lax.psum((jnp.sum(own_inside), jnp.sum(own_inside * source)), AXES)  42.2 us
    psum x1, blocking collectives, body(): sums = lax.psum(jnp.sum(dots, axis=1), AXES)  42.1 us
    pallas_call x1, Pallas kernels, body(): pl.pallas_call(functools.partial(powers_kernel, extent), out_shape=(jax.S...  32.7 us
    ppermute x4, starting transfers between devices, shifted(): return lax.ppermute(value, axis, pairs)  12.4 us
    ppermute x4, waiting for transfers between devices, shifted(): return lax.ppermute(value, axis, pairs)  9.67 us
    pallas_call x1, Pallas kernels, body(): pl.pallas_call(combine_kernel, out_shape=(jax.ShapeDtypeStruct(extent, jn...  4.62 us
  transfers between devices with their start and end apart: 6, of which 3 were waited for; matrix products, arithmetic and copies ran while one was open for 3% of the time, Pallas kernels for 0%

profile of v1, /device:TPU:0, one launch (start us, length us, event | category | flops | bytes accessed | tf_op | source)
XLA Modules:
  0.0 164.0 jit_solution(467697990444236026)
XLA Ops:
  0.6 0.9 convert_bitcast_fusion
  1.5 1.0 pad_maximum_fusion.3
  2.5 0.6 collective-permute-start.1
  3.1 0.1 collective-permute-start
  3.1 0.1 fusion.11
  3.2 0.1 fusion.21
  3.3 0.1 negate_maximum_fusion
  3.4 0.1 negate_maximum_fusion.2
  3.5 0.1 negate_maximum_fusion.3
  3.6 0.1 negate_maximum_fusion.5
  3.7 0.1 broadcast_maximum_fusion
  3.8 0.1 broadcast_maximum_fusion.2
  3.9 1.6 %convert_reduce_fusion = (f32[]{:T(128)}, f32[]{:T(128)}) fusion(f32[8,24,128]{2,1,0:T(8,128)} %param.9, s32[8,24,128]{2,1,0:T(8,128)} %param.7), kind=kLoop, calls=%fused_computation.7 | loop fusion | flops 147454 | bytes 196616 | tf_op jit(solution)/shard_map/reduce_sum | solution.py:294
  5.6 0.6 pad.13.clone
  6.2 42.2 %all-reduce.1 = (f32[]{:T(128)}, f32[]{:T(128)}) all-reduce(f32[]{:T(128)} %get-tuple-element.21, f32[]{:T(128)} %get-tuple-element.20), channel_id=1, replica_groups=mesh['gx'=4,'gy'=4,'gz'=2] {'gx','gy','gz'}, use_global_device_ids=true, to_apply=%region_2.0 | all-reduce | flops 2 | bytes 16 | tf_op jit(solution)/shard_map/psum | solution.py:293
  49.5 0.1 broadcast_maximum_fusion.4
  49.6 0.1 concatenate.21
  49.7 0.0 collective-permute-done
  49.7 0.7 pad_add_fusion
  50.5 0.0 collective-permute-done.1
  50.5 1.0 pad_maximum_fusion.2
  51.5 0.0 copy-start
  51.5 0.0 copy-start.2
  51.5 0.1 fusion.29
  51.5 1.3 collective-permute-start.2
  52.8 4.6 %collective-permute-start.3 = (f32[16,3,9,128]{3,2,0,1:T(8,128)S(1)}, f32[16,3,9,128]{3,2,0,1:T(8,128)S(1)}, u32[]{:S(2)}, u32[]{:S(2)}) collective-permute-start(f32[16,3,9,128]{3,2,0,1:T(8,128)S(1)} %get-tuple-element.30), channel_id=1, source_target_pairs={{0,8},{8,16},{16,24},{1,9},{9,17},{17,25},{2,10},{10,18},{18,26},{... | collective-permute-start | bytes 663560 | tf_op jit(solution)/shard_map/ppermute | solution.py:65
  57.4 0.2 fusion.7
  57.6 6.1 %collective-permute-done.2 = f32[16,3,9,128]{3,2,0,1:T(8,128)S(1)} collective-permute-done((f32[16,3,9,128]{3,2,0,1:T(8,128)S(1)}, f32[16,3,9,128]{3,2,0,1:T(8,128)S(1)}, u32[]{:S(2)}, u32[]{:S(2)}) %collective-permute-start.2) | collective-permute-done | bytes 221216 | tf_op jit(solution)/shard_map/ppermute | solution.py:65
  63.7 1.2 collective-permute-done.3
  64.8 0.0 copy-start.1
  64.9 0.0 copy-done
  64.9 0.0 copy-done.2
  64.9 0.2 pad_maximum_fusion.1
  65.0 0.5 copy-done.1
  65.6 0.4 fusion.28
  66.0 1.1 copy.10
  67.1 1.3 collective-permute-start.4
  68.4 0.4 copy.11
  68.8 5.2 %collective-permute-start.5 = (f32[16,3,48,9]{2,0,3,1:T(8,128)S(1)}, f32[16,3,48,9]{2,0,3,1:T(8,128)}, u32[]{:S(2)}, u32[]{:S(2)}) collective-permute-start(f32[16,3,48,9]{2,0,3,1:T(8,128)S(1)} %copy.11), channel_id=1, source_target_pairs={{0,2},{2,4},{4,6},{1,3},{3,5},{5,7},{8,10},{10,12},{12,14},{9,11},... | collective-permute-start | bytes 248840 | tf_op jit(solution)/shard_map/ppermute | solution.py:65
  74.1 0.7 pad_maximum_fusion.4.table
  74.7 0.0 copy-start.3
  74.7 2.4 %collective-permute-done.4 = f32[16,3,48,9]{2,0,3,1:T(8,128)S(1)} collective-permute-done((f32[16,3,48,9]{2,0,3,1:T(8,128)}, f32[16,3,48,9]{2,0,3,1:T(8,128)S(1)}, u32[]{:S(2)}, u32[]{:S(2)}) %collective-permute-start.4) | collective-permute-done | bytes 82976 | tf_op jit(solution)/shard_map/ppermute | solution.py:65
  77.2 0.4 copy.12
  77.6 0.0 collective-permute-done.5
  77.6 1.4 copy.13
  79.0 0.0 copy-done.3
  79.0 1.5 pad_maximum_fusion
  80.6 1.4 slice_bitcast_fusion
  82.0 32.7 %shard_map.59 = (f32[9,8,24,128]{3,2,1,0:T(8,128)}, f32[8,24,128]{2,1,0:T(8,128)}, f32[24,128]{1,0:T(8,128)}) custom-call(f32[16,19]{1,0:T(8,128)} %pad_maximum_fusion.4.table, f32[1]{0:T(128)} %bitcast.stats, f32[16,48,256]{2,1,0:T(8,128)} %get-tuple-element.26.mask, f32[16,48,256]{2,1,0:T(8,128)} %get-tuple-element.25.potential, ...), custom_call_target="tpu_custom_call" | custom-call | tf_op jit(solution)/shard_map/pallas_call | solution.py:322
  114.7 0.8 reduce_sum.29
  115.5 0.6 compare_reduce_fusion
  116.1 42.1 %psum.23 = f32[24]{0:T(128)S(1)} all-reduce(f32[24]{0:T(128)S(1)} %reduce_sum.29), channel_id=1, replica_groups=mesh['gx'=4,'gy'=4,'gz'=2] {'gx','gy','gz'}, use_global_device_ids=true, to_apply=%region_6.7 | all-reduce | flops 24 | bytes 192 | tf_op jit(solution)/shard_map/psum | solution.py:335
  158.2 0.6 fusion.25
  158.9 0.5 scatter.4.raw
  159.4 4.6 %shard_map.60 = (f32[8,24,128]{2,1,0:T(8,128)}, f32[8,24,128]{2,1,0:T(8,128)}) custom-call(f32[1,128]{1,0:T(1,128)} %scatter.4.raw, f32[1]{0:T(128)} %bitcast.8.count, f32[9,8,24,128]{3,2,1,0:T(8,128)} %get-tuple-element.18.basis, f32[8,24,128]{2,1,0:T(8,128)} %get-tuple-element.19.scale), custom_call_target="tpu_custom_call" | custom-call | tf_op jit(solution)/shard_map/pallas_call | solution.py:338
  (3 shorter events, 0.0 us)
Async XLA Ops:
  2.5 48.0 %collective-permute-start.1 = (f32[8,3,24,128]{3,2,0,1:T(8,128)S(1)}, f32[8,3,24,128]{3,2,0,1:T(8,128)S(1)}, u32[]{:S(2)}, u32[]{:S(2)}) collective-permute-start(f32[8,3,24,128]{3,2,0,1:T(8,128)S(1)} %pad_maximum_fusion.3), channel_id=1, source_target_pairs={{0,1},{1,0},{2,3},{3,2},{4,5},{5,4},{6,7},{7,6},{8,9},{9,8},{10,11... | collective-permute-start | bytes 884744 | tf_op jit(solution)/shard_map/ppermute | solution.py:73
  3.1 46.7 %collective-permute-start = (s32[8]{0:T(128)}, s32[8]{0:T(128)S(1)}, u32[]{:S(2)}, u32[]{:S(2)}) collective-permute-start(s32[8]{0:T(128)} %param.8), channel_id=1, source_target_pairs={{0,1},{1,0},{2,3},{3,2},{4,5},{5,4},{6,7},{7,6},{8,9},{9,8},{10,11... | collective-permute-start | bytes 104 | tf_op jit(solution)/shard_map/ppermute | solution.py:73
  51.5 13.4 %copy-start = (f32[8,24,128]{2,1,0:T(8,128)S(1)}, f32[8,24,128]{2,1,0:T(8,128)}, u32[]{:S(2)}) copy-start(f32[8,24,128]{2,1,0:T(8,128)} %param.9) | copy-start | bytes 294916
  51.5 13.4 %copy-start.2 = (f32[8,24,128]{2,1,0:T(8,128)S(1)}, f32[8,24,128]{2,1,0:T(8,128)}, u32[]{:S(2)}) copy-start(f32[8,24,128]{2,1,0:T(8,128)} %param.6) | copy-start | bytes 294916
  51.5 12.1 %collective-permute-start.2 = (f32[16,3,9,128]{3,2,0,1:T(8,128)S(1)}, f32[16,3,9,128]{3,2,0,1:T(8,128)S(1)}, u32[]{:S(2)}, u32[]{:S(2)}) collective-permute-start(f32[16,3,9,128]{3,2,0,1:T(8,128)S(1)} %get-tuple-element.29), channel_id=1, source_target_pairs={{8,0},{16,8},{24,16},{9,1},{17,9},{25,17},{10,2},{18,10},{26,18},{... | collective-permute-start | bytes 663560 | tf_op jit(solution)/shard_map/ppermute | solution.py:65
  52.8 12.0 %collective-permute-start.3 = (f32[16,3,9,128]{3,2,0,1:T(8,128)S(1)}, f32[16,3,9,128]{3,2,0,1:T(8,128)S(1)}, u32[]{:S(2)}, u32[]{:S(2)}) collective-permute-start(f32[16,3,9,128]{3,2,0,1:T(8,128)S(1)} %get-tuple-element.30), channel_id=1, source_target_pairs={{0,8},{8,16},{16,24},{1,9},{9,17},{17,25},{2,10},{10,18},{18,26},{... | collective-permute-start | bytes 663560 | tf_op jit(solution)/shard_map/ppermute | solution.py:65
  64.8 0.7 copy-start.1
  67.1 10.1 %collective-permute-start.4 = (f32[16,3,48,9]{2,0,3,1:T(8,128)}, f32[16,3,48,9]{2,0,3,1:T(8,128)S(1)}, u32[]{:S(2)}, u32[]{:S(2)}) collective-permute-start(f32[16,3,48,9]{2,0,3,1:T(8,128)} %copy.10), channel_id=1, source_target_pairs={{2,0},{4,2},{6,4},{3,1},{5,3},{7,5},{10,8},{12,10},{14,12},{11,9},... | collective-permute-start | bytes 248840 | tf_op jit(solution)/shard_map/ppermute | solution.py:65
  68.8 8.8 %collective-permute-start.5 = (f32[16,3,48,9]{2,0,3,1:T(8,128)S(1)}, f32[16,3,48,9]{2,0,3,1:T(8,128)}, u32[]{:S(2)}, u32[]{:S(2)}) collective-permute-start(f32[16,3,48,9]{2,0,3,1:T(8,128)S(1)} %copy.11), channel_id=1, source_target_pairs={{0,2},{2,4},{4,6},{1,3},{3,5},{5,7},{8,10},{10,12},{12,14},{9,11},... | collective-permute-start | bytes 248840 | tf_op jit(solution)/shard_map/ppermute | solution.py:65
  74.7 4.3 %copy-start.3 = (f32[256]{0:T(256)S(1)}, f32[256]{0:T(256)}, u32[]{:S(2)}) copy-start(f32[256]{0:T(256)} %pad.13.clone) | copy-start | bytes 3076

commit v2 on v1

--- a/solution.py
+++ b/solution.py
@@ -123,11 +123,75 @@
     SLOT[tuple(-o for o in _offset)] = (_column, 2 * _column + 1)
 
 
-def powers_kernel(extent, table, stats, mask, potential, source, basis, scale, dots,
-                  weights, spare, first, second, jac):
+def grid_kernel(extent, sizes, table, mask, potential, source, phi, residual,
+                basis, scale, dots, weights, spare, first, second, jac,
+                own_row, early, final_row, late, sends, early_recv, late_recv):
     planes, rows, lanes = mask.shape
     nz, nx, ny = extent
-    mean_rhs = stats[0]
+    peers = math.prod(sizes)
+    me = 0
+    for axis, size in zip(AXES, sizes):
+        me = me * size + lax.axis_index(axis)
+
+    def device(index):
+        return (index // (sizes[1] * sizes[2]), index // sizes[2] % sizes[1], index % sizes[2])
+
+    def peer(k):
+        return lax.rem(me + k, peers)
+
+    barrier = pltpu.get_barrier_semaphore()
+
+    def greet(k, carry):
+        pl.semaphore_signal(
+            barrier, inc=1, device_id=device(peer(k)), device_id_type=pl.DeviceIdType.MESH
+        )
+        return carry
+
+    lax.fori_loop(1, peers, greet, 0)
+
+    def spread(row, gathered, recv):
+        def one(k, carry):
+            pltpu.make_async_remote_copy(
+                src_ref=row, dst_ref=gathered.at[me], send_sem=sends.at[k],
+                recv_sem=recv.at[me], device_id=device(peer(k)),
+                device_id_type=pl.DeviceIdType.MESH,
+            ).start()
+            return carry
+
+        lax.fori_loop(1, peers, one, 0)
+
+    def collect(row, gathered, recv):
+        def one(k, carry):
+            other = peer(k)
+            copy = pltpu.make_async_remote_copy(
+                src_ref=row, dst_ref=gathered.at[other], send_sem=sends.at[k],
+                recv_sem=recv.at[other], device_id=device(other),
+                device_id_type=pl.DeviceIdType.MESH,
+            )
+            copy.wait_recv()
+            copy.wait_send()
+            return carry
+
+        lax.fori_loop(1, peers, one, 0)
+        gathered[me] = row[...]
+        return jnp.sum(gathered[...], axis=0)
+
+    lane = lax.broadcasted_iota(jnp.int32, (1, 128), 1)
+
+    def pick(vector, index):
+        return jnp.sum(jnp.where(lane == index, vector, 0.0), axis=1, keepdims=True)
+
+    cells = jnp.zeros((1, ny), jnp.float32)
+    injected = jnp.zeros((1, ny), jnp.float32)
+    for plane in range(nz):
+        own_inside = jnp.where(mask[plane, 0:nx, 0:ny] > 0.0, 1.0, 0.0)
+        cells = cells + jnp.sum(own_inside, axis=0, keepdims=True)
+        injected = injected + jnp.sum(
+            own_inside * source[plane, 0:nx, 0:ny], axis=0, keepdims=True
+        )
+    cells = jnp.sum(cells, axis=1, keepdims=True)
+    injected = jnp.sum(injected, axis=1, keepdims=True)
+    own_row[...] = jnp.where(lane == 0, cells, jnp.where(lane == 1, injected, 0.0))
 
     def neighbours(plane):
         above = jnp.where(plane + 1 == planes, 0, plane + 1)
@@ -175,7 +239,7 @@
         jacobi = inside / bounded
         jac[plane] = jacobi + jacobi
         spare[plane] = inside * (1.0 - jacobi * total)
-        first[plane] = jacobi * (inside * source[plane] - image - inside * mean_rhs)
+        first[plane] = jacobi * (inside * source[plane] - image)
 
         @pl.when(plane < nz)
         def _():
@@ -183,7 +247,19 @@
 
         return carry
 
-    lax.fori_loop(0, planes, setup, 0)
+    lax.fori_loop(0, planes // 2, setup, 0)
+    pl.semaphore_wait(barrier, peers - 1)
+    spread(own_row, early, early_recv)
+    lax.fori_loop(planes // 2, planes, setup, 0)
+    totals = collect(own_row, early, early_recv)
+    count = pick(totals, 0)
+    mean_rhs = pick(totals, 1) / count
+
+    def centre(plane, carry):
+        first[plane] = first[plane] - 0.5 * jac[plane] * mean_rhs
+        return carry
+
+    lax.fori_loop(0, planes, centre, 0)
 
     def record(step, now, before):
         rowsum = jnp.zeros((1, ny), jnp.float32)
@@ -227,14 +303,13 @@
         now, old = old, now
         record(step, now, old)
 
-
-def combine_kernel(raw, count, basis, scale, phi, residual):
-    nz = scale.shape[0]
-    lane = lax.broadcasted_iota(jnp.int32, (1, 128), 1)
-    sums = raw[...]
-
-    def pick(vector, index):
-        return jnp.sum(jnp.where(lane == index, vector, 0.0), axis=1, keepdims=True)
+    partial = jnp.sum(dots[...], axis=1, keepdims=True)
+    diagonal = lax.broadcasted_iota(jnp.int32, (3 * ITERS, 128), 0) == lax.broadcasted_iota(
+        jnp.int32, (3 * ITERS, 128), 1
+    )
+    final_row[...] = jnp.sum(jnp.where(diagonal, partial, 0.0), axis=0, keepdims=True)
+    spread(final_row, late, late_recv)
+    sums = collect(final_row, late, late_recv)
 
     def left(vector):
         return pltpu.roll(vector, 127, 1)
@@ -266,7 +341,7 @@
             p = y + beta * p
             m_p = m_y + beta * m_p
             rz = rz_next
-    mean = jnp.sum(jnp.where(lane < ITERS, x * ones, 0.0), axis=1, keepdims=True) / count[0]
+    mean = jnp.sum(jnp.where(lane < ITERS, x * ones, 0.0), axis=1, keepdims=True) / count
     xs = [pick(x, j) for j in range(ITERS)]
     ys = [pick(y, j) for j in range(ITERS + 1)]
 
@@ -289,10 +364,6 @@
     extent = tissue_mask.shape
     nz = extent[0]
     labels = tissue_mask.astype(jnp.float32)
-    own_inside = (labels > 0.0).astype(jnp.float32)
-    count, rhs_total = lax.psum(
-        (jnp.sum(own_inside), jnp.sum(own_inside * source)), AXES
-    )
     packed = jnp.stack([labels, potential, source], axis=1)
     packed = framed(packed, "gz", 0, 1)
     packed = framed(packed, "gx", 2, 8)
@@ -319,28 +390,29 @@
     frame = (planes,) + packed.shape[2:]
     smem = pl.BlockSpec(memory_space=pltpu.SMEM)
     vmem = pl.BlockSpec(memory_space=pltpu.VMEM)
-    basis, scale, dots = pl.pallas_call(
-        functools.partial(powers_kernel, extent),
-        out_shape=(
-            jax.ShapeDtypeStruct((ITERS + 1,) + extent, jnp.float32),
-            jax.ShapeDtypeStruct(extent, jnp.float32),
-            jax.ShapeDtypeStruct((3 * ITERS, extent[2]), jnp.float32),
-        ),
-        in_specs=[smem, smem, vmem, vmem, vmem],
-        out_specs=(vmem, vmem, vmem),
-        scratch_shapes=[pltpu.VMEM((18,) + frame, jnp.float32)]
-        + [pltpu.VMEM(frame, jnp.float32)] * 4,
-        compiler_params=pltpu.CompilerParams(vmem_limit_bytes=60 * 1024 * 1024),
-    )(table, (rhs_total / count)[None], packed[:, 0], packed[:, 1], packed[:, 2])
-    sums = lax.psum(jnp.sum(dots, axis=1), AXES)
-    raw = jnp.zeros((1, 128), jnp.float32).at[0, : 3 * ITERS].set(sums)
+    sizes = tuple(lax.axis_size(axis) for axis in AXES)
+    peers = math.prod(sizes)
+    row = pltpu.VMEM((1, 128), jnp.float32)
+    gathered = pltpu.VMEM((peers, 1, 128), jnp.float32)
     return tuple(
         pl.pallas_call(
-            combine_kernel,
+            functools.partial(grid_kernel, extent, sizes),
             out_shape=(jax.ShapeDtypeStruct(extent, jnp.float32),) * 2,
-            in_specs=[vmem, smem, vmem, vmem],
+            in_specs=[smem, vmem, vmem, vmem],
             out_specs=(vmem, vmem),
-        )(raw, count[None], basis, scale)
+            scratch_shapes=[
+                pltpu.VMEM((ITERS + 1,) + extent, jnp.float32),
+                pltpu.VMEM(extent, jnp.float32),
+                pltpu.VMEM((3 * ITERS, extent[2]), jnp.float32),
+                pltpu.VMEM((18,) + frame, jnp.float32),
+            ]
+            + [pltpu.VMEM(frame, jnp.float32)] * 4
+            + [row, gathered, row, gathered]
+            + [pltpu.SemaphoreType.DMA((peers,))] * 3,
+            compiler_params=pltpu.CompilerParams(
+                vmem_limit_bytes=60 * 1024 * 1024, collective_id=0, has_side_effects=True
+            ),
+        )(table, packed[:, 0], packed[:, 1], packed[:, 2])
     )
 
 

time: 165 us -> 92.5 us (0.56)
  blocking collectives: 84.3 us -> 0 us
  Pallas kernels: 37.3 us -> 50.2 us
  other arithmetic: 10.6 us -> 6.8 us
  local copies, waits for them, and re-layouts: 7.06 us -> 9.65 us
    psum x2 -> x0, blocking collectives: 84.3 us -> none  [the longest x1 42.2 us: body(): lax.psum((jnp.sum(own_inside), jnp.sum(own_inside * source)), AXES)]
    pallas_call x2 -> x1, Pallas kernels: 37.3 us -> 50.2 us  [body(): pl.pallas_call(functools.partial(grid_kernel, extent, sizes), out_shape=(...]
    unnamed x8 -> x10, local copies, waits for them, and re-layouts: 0.55 us -> 3.64 us
    reduce_sum x2 -> x0, other arithmetic: 2.46 us -> none  [the longest x1 1.64 us: body(): jnp.sum(own_inside)]
  transfers between devices with their start and end apart: 6 -> 6, of which waited for: 3 -> 4; matrix products, arithmetic and copies ran while one was open for 3% -> 4% of each run, Pallas kernels for 0% -> 0%
where the time goes in v2:
time: 92.5 us; the launch traced here: 92 us
  Pallas kernels  50.2 us (54%)
  starting transfers between devices  14 us (15%)
  waiting for transfers between devices  10.4 us (11%)
  local copies, waits for them, and re-layouts  9.65 us (10%)
  other arithmetic  6.8 us (7%)
    pallas_call x1, Pallas kernels, body(): pl.pallas_call(functools.partial(grid_kernel, extent, sizes), out_shape=(...  50.2 us
    ppermute x4, starting transfers between devices, shifted(): return lax.ppermute(value, axis, pairs)  13.4 us
    ppermute x4, waiting for transfers between devices, shifted(): return lax.ppermute(value, axis, pairs)  10.4 us
    unnamed x10, local copies, waits for them, and re-layouts  3.64 us
    another operation x2, other arithmetic, body(): packed = jnp.stack([labels, potential, source], axis=1)  1.86 us
  transfers between devices with their start and end apart: 6, of which 4 were waited for; matrix products, arithmetic and copies ran while one was open for 4% of the time, Pallas kernels for 0%

profile of v2, /device:TPU:0, one launch (start us, length us, event | category | flops | bytes accessed | tf_op | source)
XLA Modules:
  0.0 92.0 jit_solution(12394115045421086261)
XLA Ops:
  0.6 0.9 convert_bitcast_fusion
  1.5 1.0 %pad_maximum_fusion.3 = f32[8,3,24,128]{3,2,0,1:T(8,128)S(1)} fusion(f32[8,1,24,128]{3,2,0,1:T(8,128)} %bitcast.11, f32[8,1,24,128]{3,2,0,1:T(8,128)} %bitcast.15, f32[8,1,24,128]{3,2,0,1:T(8,128)S(1)} %convert_bitcast_fusion), kind=kLoop, calls=%fused_computation.6 | loop fusion | flops 147456 | bytes 589824 | tf_op jit(solution)/shard_map/stack | solution.py:367
  2.5 0.6 collective-permute-start.1
  3.1 0.1 collective-permute-start
  3.1 0.1 fusion.11
  3.2 0.1 fusion.21
  3.3 0.1 negate_maximum_fusion
  3.4 0.1 negate_maximum_fusion.2
  3.5 0.1 negate_maximum_fusion.3
  3.6 0.1 negate_maximum_fusion.5
  3.7 0.1 broadcast_maximum_fusion
  3.8 0.1 broadcast_maximum_fusion.2
  3.9 0.6 pad.8.clone
  4.6 0.1 broadcast_maximum_fusion.4
  4.7 0.1 concatenate.19
  4.8 0.0 collective-permute-done
  4.8 0.7 pad_add_fusion
  5.5 0.0 collective-permute-done.1
  5.5 1.0 %pad_maximum_fusion.2 = f32[16,3,24,128]{3,2,0,1:T(8,128)S(1)} fusion(f32[8,3,24,128]{3,2,0,1:T(8,128)S(1)} %collective-permute-done.1, f32[8,1,24,128]{3,2,0,1:T(8,128)} %bitcast.12, f32[8,1,24,128]{3,2,0,1:T(8,128)} %bitcast.16, f32[8,1,24,128]{3,2,0,1:T(8,128)S(1)} %convert_bitcast_fusion), kind=kLoop, calls=%fused_computation.5 | loop fusion | flops 442368 | bytes 1179648 | tf_op jit(solution)/shard_map/concatenate | solution.py:74
  6.5 0.0 copy-start.1
  6.5 0.0 copy-start.2
  6.5 0.1 fusion.28
  6.6 1.3 %collective-permute-start.2 = (f32[16,3,9,128]{3,2,0,1:T(8,128)S(1)}, f32[16,3,9,128]{3,2,0,1:T(8,128)S(1)}, u32[]{:S(2)}, u32[]{:S(2)}) collective-permute-start(f32[16,3,9,128]{3,2,0,1:T(8,128)S(1)} %get-tuple-element.7), channel_id=1, source_target_pairs={{8,0},{16,8},{24,16},{9,1},{17,9},{25,17},{10,2},{18,10},{26,18},{... | collective-permute-start | bytes 663560 | tf_op jit(solution)/shard_map/ppermute | solution.py:65
  7.9 5.5 %collective-permute-start.3 = (f32[16,3,9,128]{3,2,0,1:T(8,128)S(1)}, f32[16,3,9,128]{3,2,0,1:T(8,128)S(1)}, u32[]{:S(2)}, u32[]{:S(2)}) collective-permute-start(f32[16,3,9,128]{3,2,0,1:T(8,128)S(1)} %get-tuple-element.8), channel_id=1, source_target_pairs={{0,8},{8,16},{16,24},{1,9},{9,17},{17,25},{2,10},{10,18},{18,26},{... | collective-permute-start | bytes 663560 | tf_op jit(solution)/shard_map/ppermute | solution.py:65
  13.4 0.2 fusion.7
  13.6 7.2 %collective-permute-done.2 = f32[16,3,9,128]{3,2,0,1:T(8,128)S(1)} collective-permute-done((f32[16,3,9,128]{3,2,0,1:T(8,128)S(1)}, f32[16,3,9,128]{3,2,0,1:T(8,128)S(1)}, u32[]{:S(2)}, u32[]{:S(2)}) %collective-permute-start.2) | collective-permute-done | bytes 221216 | tf_op jit(solution)/shard_map/ppermute | solution.py:65
  20.8 1.2 %collective-permute-done.3 = f32[16,3,9,128]{3,2,0,1:T(8,128)S(1)} collective-permute-done((f32[16,3,9,128]{3,2,0,1:T(8,128)S(1)}, f32[16,3,9,128]{3,2,0,1:T(8,128)S(1)}, u32[]{:S(2)}, u32[]{:S(2)}) %collective-permute-start.3) | collective-permute-done | bytes 221216 | tf_op jit(solution)/shard_map/ppermute | solution.py:65
  22.0 0.0 copy-start
  22.0 0.0 copy-done.1
  22.0 0.0 copy-done.2
  22.1 0.2 pad_maximum_fusion.1
  22.2 0.5 copy-done
  22.8 0.4 fusion.27
  23.2 1.1 %copy.10 = f32[16,3,48,9]{2,0,3,1:T(8,128)} copy(f32[16,3,48,9]{3,2,0,1:T(8,128)S(1)} %get-tuple-element.5) | data formatting | bytes 165888 | tf_op jit(solution)/shard_map/slice | solution.py:81
  24.3 1.3 %collective-permute-start.4 = (f32[16,3,48,9]{2,0,3,1:T(8,128)}, f32[16,3,48,9]{2,0,3,1:T(8,128)S(1)}, u32[]{:S(2)}, u32[]{:S(2)}) collective-permute-start(f32[16,3,48,9]{2,0,3,1:T(8,128)} %copy.10), channel_id=1, source_target_pairs={{2,0},{4,2},{6,4},{3,1},{5,3},{7,5},{10,8},{12,10},{14,12},{11,9},... | collective-permute-start | bytes 248840 | tf_op jit(solution)/shard_map/ppermute | solution.py:65
  25.6 0.4 copy.11
  26.0 5.2 %collective-permute-start.5 = (f32[16,3,48,9]{2,0,3,1:T(8,128)S(1)}, f32[16,3,48,9]{2,0,3,1:T(8,128)}, u32[]{:S(2)}, u32[]{:S(2)}) collective-permute-start(f32[16,3,48,9]{2,0,3,1:T(8,128)S(1)} %copy.11), channel_id=1, source_target_pairs={{0,2},{2,4},{4,6},{1,3},{3,5},{5,7},{8,10},{10,12},{12,14},{9,11},... | collective-permute-start | bytes 248840 | tf_op jit(solution)/shard_map/ppermute | solution.py:65
  31.2 0.7 pad_maximum_fusion.4.table
  31.9 0.0 copy-start.3
  31.9 1.6 %collective-permute-done.4 = f32[16,3,48,9]{2,0,3,1:T(8,128)S(1)} collective-permute-done((f32[16,3,48,9]{2,0,3,1:T(8,128)}, f32[16,3,48,9]{2,0,3,1:T(8,128)S(1)}, u32[]{:S(2)}, u32[]{:S(2)}) %collective-permute-start.4) | collective-permute-done | bytes 82976 | tf_op jit(solution)/shard_map/ppermute | solution.py:65
  33.5 0.4 copy.12
  34.0 0.4 collective-permute-done.5
  34.3 1.4 %copy.13 = f32[16,3,48,9]{3,2,0,1:T(8,128)S(1)} copy(f32[16,3,48,9]{2,0,3,1:T(8,128)} %collective-permute-done.5) | data formatting | bytes 165888 | tf_op jit(solution)/shard_map/ppermute | solution.py:65
  35.7 0.0 copy-done.3
  35.7 1.5 %pad_maximum_fusion = f32[16,3,48,256]{3,2,0,1:T(8,128)S(1)} fusion(f32[16,3,48,9]{3,2,0,1:T(8,128)S(1)} %copy.13, f32[16,3,48,9]{3,2,0,1:T(8,128)S(1)} %copy.12, f32[16,3,9,128]{3,2,0,1:T(8,128)} %copy-done, f32[16,3,6,128]{3,2,0,1:T(8,128)S(1)} %broadcast_in_dim.4, f32[16,3,9,128]{3,2,0,1:T(8,128)S(1)} %collective-permute-done.2, ...), kind=kLoop, calls=%fused_computation | loop fusion | flops 5308416 | bytes 3705856 | tf_op jit(solution)/shard_map/concatenate | solution.py:96
  37.3 1.5 %slice_bitcast_fusion = (f32[16,48,256]{2,1,0:T(8,128)}, f32[16,48,256]{2,1,0:T(8,128)}, f32[16,48,256]{2,1,0:T(8,128)}) fusion(f32[16,3,48,256]{3,2,0,1:T(8,128)S(1)} %pad_maximum_fusion), kind=kLoop, calls=%fused_computation.2 | loop fusion | bytes 4718592 | tf_op jit(solution)/shard_map/squeeze | solution.py:415
  38.7 50.2 %shard_map.59 = (f32[8,24,128]{2,1,0:T(8,128)}, f32[8,24,128]{2,1,0:T(8,128)}) custom-call(f32[16,19]{1,0:T(8,128)} %pad_maximum_fusion.4.table, f32[16,48,256]{2,1,0:T(8,128)} %get-tuple-element.4.mask, f32[16,48,256]{2,1,0:T(8,128)} %get-tuple-element.3.potential, f32[16,48,256]{2,1,0:T(8,128)} %get-tuple-element.2.source), custom_call_target="tpu_custom_call" | custom-call | tf_op jit(solution)/shard_map/pallas_call | solution.py:398
  88.9 1.5 %copy.16 = f32[8,24,128]{2,1,0:T(8,128)} copy(f32[8,24,128]{2,1,0:T(8,128)} %get-tuple-element.29) | data formatting | bytes 196608
  90.5 1.5 %copy.17 = f32[8,24,128]{2,1,0:T(8,128)} copy(f32[8,24,128]{2,1,0:T(8,128)} %get-tuple-element.30) | data formatting | bytes 196608
  (3 shorter events, 0.0 us)
Async XLA Ops:
  2.5 3.0 %collective-permute-start.1 = (f32[8,3,24,128]{3,2,0,1:T(8,128)S(1)}, f32[8,3,24,128]{3,2,0,1:T(8,128)S(1)}, u32[]{:S(2)}, u32[]{:S(2)}) collective-permute-start(f32[8,3,24,128]{3,2,0,1:T(8,128)S(1)} %pad_maximum_fusion.3), channel_id=1, source_target_pairs={{0,1},{1,0},{2,3},{3,2},{4,5},{5,4},{6,7},{7,6},{8,9},{9,8},{10,11... | collective-permute-start | bytes 884744 | tf_op jit(solution)/shard_map/ppermute | solution.py:73
  3.1 1.7 %collective-permute-start = (s32[8]{0:T(128)}, s32[8]{0:T(128)S(1)}, u32[]{:S(2)}, u32[]{:S(2)}) collective-permute-start(s32[8]{0:T(128)} %param.6), channel_id=1, source_target_pairs={{0,1},{1,0},{2,3},{3,2},{4,5},{5,4},{6,7},{7,6},{8,9},{9,8},{10,11... | collective-permute-start | bytes 104 | tf_op jit(solution)/shard_map/ppermute | solution.py:73
  6.5 15.5 %copy-start.1 = (f32[8,24,128]{2,1,0:T(8,128)S(1)}, f32[8,24,128]{2,1,0:T(8,128)}, u32[]{:S(2)}) copy-start(f32[8,24,128]{2,1,0:T(8,128)} %param.7) | copy-start | bytes 294916
  6.5 15.5 %copy-start.2 = (f32[8,24,128]{2,1,0:T(8,128)S(1)}, f32[8,24,128]{2,1,0:T(8,128)}, u32[]{:S(2)}) copy-start(f32[8,24,128]{2,1,0:T(8,128)} %param.4) | copy-start | bytes 294916
  6.6 14.2 %collective-permute-start.2 = (f32[16,3,9,128]{3,2,0,1:T(8,128)S(1)}, f32[16,3,9,128]{3,2,0,1:T(8,128)S(1)}, u32[]{:S(2)}, u32[]{:S(2)}) collective-permute-start(f32[16,3,9,128]{3,2,0,1:T(8,128)S(1)} %get-tuple-element.7), channel_id=1, source_target_pairs={{8,0},{16,8},{24,16},{9,1},{17,9},{25,17},{10,2},{18,10},{26,18},{... | collective-permute-start | bytes 663560 | tf_op jit(solution)/shard_map/ppermute | solution.py:65
  7.9 14.1 %collective-permute-start.3 = (f32[16,3,9,128]{3,2,0,1:T(8,128)S(1)}, f32[16,3,9,128]{3,2,0,1:T(8,128)S(1)}, u32[]{:S(2)}, u32[]{:S(2)}) collective-permute-start(f32[16,3,9,128]{3,2,0,1:T(8,128)S(1)} %get-tuple-element.8), channel_id=1, source_target_pairs={{0,8},{8,16},{16,24},{1,9},{9,17},{17,25},{2,10},{10,18},{18,26},{... | collective-permute-start | bytes 663560 | tf_op jit(solution)/shard_map/ppermute | solution.py:65
  22.0 0.8 copy-start
  24.3 9.2 %collective-permute-start.4 = (f32[16,3,48,9]{2,0,3,1:T(8,128)}, f32[16,3,48,9]{2,0,3,1:T(8,128)S(1)}, u32[]{:S(2)}, u32[]{:S(2)}) collective-permute-start(f32[16,3,48,9]{2,0,3,1:T(8,128)} %copy.10), channel_id=1, source_target_pairs={{2,0},{4,2},{6,4},{3,1},{5,3},{7,5},{10,8},{12,10},{14,12},{11,9},... | collective-permute-start | bytes 248840 | tf_op jit(solution)/shard_map/ppermute | solution.py:65
  26.0 8.3 %collective-permute-start.5 = (f32[16,3,48,9]{2,0,3,1:T(8,128)S(1)}, f32[16,3,48,9]{2,0,3,1:T(8,128)}, u32[]{:S(2)}, u32[]{:S(2)}) collective-permute-start(f32[16,3,48,9]{2,0,3,1:T(8,128)S(1)} %copy.11), channel_id=1, source_target_pairs={{0,2},{2,4},{4,6},{1,3},{3,5},{5,7},{8,10},{10,12},{12,14},{9,11},... | collective-permute-start | bytes 248840 | tf_op jit(solution)/shard_map/ppermute | solution.py:65
  31.9 3.8 %copy-start.3 = (f32[256]{0:T(256)S(1)}, f32[256]{0:T(256)}, u32[]{:S(2)}) copy-start(f32[256]{0:T(256)} %pad.8.clone) | copy-start | bytes 3076

commit v3 on v2

--- a/solution.py
+++ b/solution.py
@@ -128,6 +128,8 @@
                 own_row, early, final_row, late, sends, early_recv, late_recv):
     planes, rows, lanes = mask.shape
     nz, nx, ny = extent
+    held = jac.shape[1]
+    keep = nx + ITERS
     peers = math.prod(sizes)
     me = 0
     for axis, size in zip(AXES, sizes):
@@ -197,6 +199,13 @@
         above = jnp.where(plane + 1 == planes, 0, plane + 1)
         below = jnp.where(plane == 0, planes - 1, plane - 1)
         return above, below
+
+    def store(ref, index, value):
+        if held == rows:
+            ref[index] = value
+        else:
+            ref[(*index, slice(0, keep))] = value[:keep]
+            ref[(*index, slice(keep, held))] = value[rows - held + keep :]
 
     def setup(plane, carry):
         above, below = neighbours(plane)
@@ -231,15 +240,15 @@
                 )
             else:
                 weight = inside * (jnp.where(label > 0.0, weight, 0.0) + their_tissue * g_there)
-            weights[slot, plane] = weight
+            store(weights, (slot, plane), weight)
             total = total + weight
             intra = (table[plane, 9 + column] + table[beyond, 9 + column]) * link
             image = image + (tissue * their_tissue * intra) * (volts - volt)
         bounded = jnp.maximum(total, 1.0)
         jacobi = inside / bounded
-        jac[plane] = jacobi + jacobi
-        spare[plane] = inside * (1.0 - jacobi * total)
-        first[plane] = jacobi * (inside * source[plane] - image)
+        store(jac, (plane,), jacobi + jacobi)
+        store(spare, (plane,), inside * (1.0 - jacobi * total))
+        store(first, (plane,), jacobi * (inside * source[plane] - image))
 
         @pl.when(plane < nz)
         def _():
@@ -281,13 +290,23 @@
 
     record(0, first, None)
 
-    def apply(now, old, start):
-        def one(plane, carry):
+    def apply(now, old, step):
+        reach = ITERS - step
+        if planes == nz:
+            begin, span = 0, nz
+        elif planes == sizes[2] * nz:
+            begin = planes - lax.axis_index("gz") * reach
+            span = min(planes, nz + reach)
+        else:
+            begin, span = planes - reach, nz + 2 * reach
+
+        def one(index, carry):
+            plane = lax.rem(begin + index, planes)
             above, below = neighbours(plane)
-            total = jnp.zeros((rows, lanes), jnp.float32)
-            for offset, value in fields_around(now, plane, above, below, rows, lanes):
+            total = jnp.zeros((held, lanes), jnp.float32)
+            for offset, value in fields_around(now, plane, above, below, held, lanes):
                 total = total + weights[SLOT[offset][1], plane] * value
-            if start:
+            if step == 1:
                 old[plane] = 0.5 * jac[plane] * total + spare[plane] * now[plane]
             else:
                 old[plane] = (
@@ -295,11 +314,11 @@
                 )
             return carry
 
-        lax.fori_loop(0, planes, one, 0)
+        lax.fori_loop(0, span, one, 0)
 
     now, old = first, second
     for step in range(1, ITERS + 1):
-        apply(now, old, step == 1)
+        apply(now, old, step)
         now, old = old, now
         record(step, now, old)
 
@@ -390,6 +409,9 @@
     frame = (planes,) + packed.shape[2:]
     smem = pl.BlockSpec(memory_space=pltpu.SMEM)
     vmem = pl.BlockSpec(memory_space=pltpu.VMEM)
+    compact = frame
+    if extent[1] % 8 == 0 and ITERS % 8 == 0 and frame[1] > extent[1] + 2 * ITERS:
+        compact = (planes, extent[1] + 2 * ITERS, frame[2])
     sizes = tuple(lax.axis_size(axis) for axis in AXES)
     peers = math.prod(sizes)
     row = pltpu.VMEM((1, 128), jnp.float32)
@@ -404,9 +426,9 @@
                 pltpu.VMEM((ITERS + 1,) + extent, jnp.float32),
                 pltpu.VMEM(extent, jnp.float32),
                 pltpu.VMEM((3 * ITERS, extent[2]), jnp.float32),
-                pltpu.VMEM((18,) + frame, jnp.float32),
+                pltpu.VMEM((18,) + compact, jnp.float32),
             ]
-            + [pltpu.VMEM(frame, jnp.float32)] * 4
+            + [pltpu.VMEM(compact, jnp.float32)] * 4
             + [row, gathered, row, gathered]
             + [pltpu.SemaphoreType.DMA((peers,))] * 3,
             compiler_params=pltpu.CompilerParams(

time: 92.5 us -> 83.5 us (0.903)
  Pallas kernels: 50.2 us -> 41.3 us
    pallas_call x1, Pallas kernels: 50.2 us -> 41.3 us  [body(): pl.pallas_call(functools.partial(grid_kernel, extent, sizes), out_shape=(...]
  transfers between devices with their start and end apart: 6 -> 6, of which waited for: 4 -> 4; matrix products, arithmetic and copies ran while one was open for 4% -> 5% of each run, Pallas kernels for 0% -> 0%
where the time goes in v3:
time: 83.5 us; the launch traced here: 83.1 us
  Pallas kernels  41.3 us (49%)
  starting transfers between devices  14 us (17%)
  waiting for transfers between devices  10.4 us (12%)
  local copies, waits for them, and re-layouts  9.65 us (12%)
  other arithmetic  6.8 us (8%)
    pallas_call x1, Pallas kernels, body(): pl.pallas_call(functools.partial(grid_kernel, extent, sizes), out_shape=(...  41.3 us
    ppermute x4, starting transfers between devices, shifted(): return lax.ppermute(value, axis, pairs)  13.4 us
    ppermute x4, waiting for transfers between devices, shifted(): return lax.ppermute(value, axis, pairs)  10.4 us
    unnamed x10, local copies, waits for them, and re-layouts  3.64 us
    another operation x2, other arithmetic, body(): packed = jnp.stack([labels, potential, source], axis=1)  1.86 us
    ppermute x2, local copies, waits for them, and re-layouts, shifted(): return lax.ppermute(value, axis, pairs)  1.82 us
    concatenate x2, other arithmetic, framed(): return jnp.concatenate([value, other], axis=dim)  1.71 us
    concatenate x2, other arithmetic, framed(): return jnp.concatenate([value] + after + middle + before, axis=dim)  1.68 us
  transfers between devices with their start and end apart: 6, of which 4 were waited for; matrix products, arithmetic and copies ran while one was open for 5% of the time, Pallas kernels for 0%

profile of v3, /device:TPU:0, one launch (start us, length us, event | category | flops | bytes accessed | tf_op | source)
XLA Modules:
  0.0 83.1 jit_solution(16878882910889611834)
XLA Ops:
  0.6 0.9 %convert_bitcast_fusion = f32[8,1,24,128]{3,2,0,1:T(8,128)S(1)} fusion(s32[8,24,128]{2,1,0:T(8,128)} %param.5), kind=kLoop, calls=%fused_computation.7 | loop fusion | flops 24576 | bytes 196608 | tf_op jit(solution)/shard_map/stack | solution.py:386
  1.5 1.0 %pad_maximum_fusion.3 = f32[8,3,24,128]{3,2,0,1:T(8,128)S(1)} fusion(f32[8,1,24,128]{3,2,0,1:T(8,128)} %bitcast.11, f32[8,1,24,128]{3,2,0,1:T(8,128)} %bitcast.15, f32[8,1,24,128]{3,2,0,1:T(8,128)S(1)} %convert_bitcast_fusion), kind=kLoop, calls=%fused_computation.6 | loop fusion | flops 147456 | bytes 589824 | tf_op jit(solution)/shard_map/stack | solution.py:386
  2.5 0.6 collective-permute-start.1
  3.1 0.1 collective-permute-start
  3.1 0.1 fusion.11
  3.2 0.1 fusion.21
  3.3 0.1 negate_maximum_fusion
  3.4 0.1 negate_maximum_fusion.2
  3.5 0.1 negate_maximum_fusion.3
  3.6 0.1 negate_maximum_fusion.5
  3.7 0.1 broadcast_maximum_fusion
  3.8 0.1 broadcast_maximum_fusion.2
  3.9 0.6 pad.8.clone
  4.6 0.1 broadcast_maximum_fusion.4
  4.7 0.1 concatenate.19
  4.8 0.0 collective-permute-done
  4.8 0.7 pad_add_fusion
  5.5 0.0 collective-permute-done.1
  5.5 1.0 %pad_maximum_fusion.2 = f32[16,3,24,128]{3,2,0,1:T(8,128)S(1)} fusion(f32[8,3,24,128]{3,2,0,1:T(8,128)S(1)} %collective-permute-done.1, f32[8,1,24,128]{3,2,0,1:T(8,128)} %bitcast.12, f32[8,1,24,128]{3,2,0,1:T(8,128)} %bitcast.16, f32[8,1,24,128]{3,2,0,1:T(8,128)S(1)} %convert_bitcast_fusion), kind=kLoop, calls=%fused_computation.5 | loop fusion | flops 442368 | bytes 1179648 | tf_op jit(solution)/shard_map/concatenate | solution.py:74
  6.5 0.0 copy-start.1
  6.5 0.0 copy-start.2
  6.5 0.1 fusion.28
  6.6 1.3 %collective-permute-start.2 = (f32[16,3,9,128]{3,2,0,1:T(8,128)S(1)}, f32[16,3,9,128]{3,2,0,1:T(8,128)S(1)}, u32[]{:S(2)}, u32[]{:S(2)}) collective-permute-start(f32[16,3,9,128]{3,2,0,1:T(8,128)S(1)} %get-tuple-element.7), channel_id=1, source_target_pairs={{8,0},{16,8},{24,16},{9,1},{17,9},{25,17},{10,2},{18,10},{26,18},{... | collective-permute-start | bytes 663560 | tf_op jit(solution)/shard_map/ppermute | solution.py:65
  7.9 5.5 %collective-permute-start.3 = (f32[16,3,9,128]{3,2,0,1:T(8,128)S(1)}, f32[16,3,9,128]{3,2,0,1:T(8,128)S(1)}, u32[]{:S(2)}, u32[]{:S(2)}) collective-permute-start(f32[16,3,9,128]{3,2,0,1:T(8,128)S(1)} %get-tuple-element.8), channel_id=1, source_target_pairs={{0,8},{8,16},{16,24},{1,9},{9,17},{17,25},{2,10},{10,18},{18,26},{... | collective-permute-start | bytes 663560 | tf_op jit(solution)/shard_map/ppermute | solution.py:65
  13.4 0.2 fusion.7
  13.6 7.2 %collective-permute-done.2 = f32[16,3,9,128]{3,2,0,1:T(8,128)S(1)} collective-permute-done((f32[16,3,9,128]{3,2,0,1:T(8,128)S(1)}, f32[16,3,9,128]{3,2,0,1:T(8,128)S(1)}, u32[]{:S(2)}, u32[]{:S(2)}) %collective-permute-start.2) | collective-permute-done | bytes 221216 | tf_op jit(solution)/shard_map/ppermute | solution.py:65
  20.8 1.2 %collective-permute-done.3 = f32[16,3,9,128]{3,2,0,1:T(8,128)S(1)} collective-permute-done((f32[16,3,9,128]{3,2,0,1:T(8,128)S(1)}, f32[16,3,9,128]{3,2,0,1:T(8,128)S(1)}, u32[]{:S(2)}, u32[]{:S(2)}) %collective-permute-start.3) | collective-permute-done | bytes 221216 | tf_op jit(solution)/shard_map/ppermute | solution.py:65
  22.0 0.0 copy-start
  22.0 0.0 copy-done.1
  22.0 0.0 copy-done.2
  22.1 0.2 pad_maximum_fusion.1
  22.2 0.5 copy-done
  22.8 0.4 fusion.27
  23.2 1.1 %copy.10 = f32[16,3,48,9]{2,0,3,1:T(8,128)} copy(f32[16,3,48,9]{3,2,0,1:T(8,128)S(1)} %get-tuple-element.5) | data formatting | bytes 165888 | tf_op jit(solution)/shard_map/slice | solution.py:81
  24.3 1.3 %collective-permute-start.4 = (f32[16,3,48,9]{2,0,3,1:T(8,128)}, f32[16,3,48,9]{2,0,3,1:T(8,128)S(1)}, u32[]{:S(2)}, u32[]{:S(2)}) collective-permute-start(f32[16,3,48,9]{2,0,3,1:T(8,128)} %copy.10), channel_id=1, source_target_pairs={{2,0},{4,2},{6,4},{3,1},{5,3},{7,5},{10,8},{12,10},{14,12},{11,9},... | collective-permute-start | bytes 248840 | tf_op jit(solution)/shard_map/ppermute | solution.py:65
  25.6 0.4 copy.11
  26.0 5.2 %collective-permute-start.5 = (f32[16,3,48,9]{2,0,3,1:T(8,128)S(1)}, f32[16,3,48,9]{2,0,3,1:T(8,128)}, u32[]{:S(2)}, u32[]{:S(2)}) collective-permute-start(f32[16,3,48,9]{2,0,3,1:T(8,128)S(1)} %copy.11), channel_id=1, source_target_pairs={{0,2},{2,4},{4,6},{1,3},{3,5},{5,7},{8,10},{10,12},{12,14},{9,11},... | collective-permute-start | bytes 248840 | tf_op jit(solution)/shard_map/ppermute | solution.py:65
  31.2 0.7 pad_maximum_fusion.4.table
  31.9 0.0 copy-start.3
  31.9 1.6 %collective-permute-done.4 = f32[16,3,48,9]{2,0,3,1:T(8,128)S(1)} collective-permute-done((f32[16,3,48,9]{2,0,3,1:T(8,128)}, f32[16,3,48,9]{2,0,3,1:T(8,128)S(1)}, u32[]{:S(2)}, u32[]{:S(2)}) %collective-permute-start.4) | collective-permute-done | bytes 82976 | tf_op jit(solution)/shard_map/ppermute | solution.py:65
  33.5 0.4 copy.12
  34.0 0.4 collective-permute-done.5
  34.3 1.4 %copy.13 = f32[16,3,48,9]{3,2,0,1:T(8,128)S(1)} copy(f32[16,3,48,9]{2,0,3,1:T(8,128)} %collective-permute-done.5) | data formatting | bytes 165888 | tf_op jit(solution)/shard_map/ppermute | solution.py:65
  35.7 0.0 copy-done.3
  35.7 1.5 %pad_maximum_fusion = f32[16,3,48,256]{3,2,0,1:T(8,128)S(1)} fusion(f32[16,3,48,9]{3,2,0,1:T(8,128)S(1)} %copy.13, f32[16,3,48,9]{3,2,0,1:T(8,128)S(1)} %copy.12, f32[16,3,9,128]{3,2,0,1:T(8,128)} %copy-done, f32[16,3,6,128]{3,2,0,1:T(8,128)S(1)} %broadcast_in_dim.4, f32[16,3,9,128]{3,2,0,1:T(8,128)S(1)} %collective-permute-done.2, ...), kind=kLoop, calls=%fused_computation | loop fusion | flops 5308416 | bytes 3705856 | tf_op jit(solution)/shard_map/concatenate | solution.py:96
  37.3 1.5 %slice_bitcast_fusion = (f32[16,48,256]{2,1,0:T(8,128)}, f32[16,48,256]{2,1,0:T(8,128)}, f32[16,48,256]{2,1,0:T(8,128)}) fusion(f32[16,3,48,256]{3,2,0,1:T(8,128)S(1)} %pad_maximum_fusion), kind=kLoop, calls=%fused_computation.2 | loop fusion | bytes 4718592 | tf_op jit(solution)/shard_map/squeeze | solution.py:437
  38.7 41.3 %shard_map.59 = (f32[8,24,128]{2,1,0:T(8,128)}, f32[8,24,128]{2,1,0:T(8,128)}) custom-call(f32[16,19]{1,0:T(8,128)} %pad_maximum_fusion.4.table, f32[16,48,256]{2,1,0:T(8,128)} %get-tuple-element.4.mask, f32[16,48,256]{2,1,0:T(8,128)} %get-tuple-element.3.potential, f32[16,48,256]{2,1,0:T(8,128)} %get-tuple-element.2.source), custom_call_target="tpu_custom_call" | custom-call | tf_op jit(solution)/shard_map/pallas_call | solution.py:420
  80.0 1.5 %copy.16 = f32[8,24,128]{2,1,0:T(8,128)} copy(f32[8,24,128]{2,1,0:T(8,128)} %get-tuple-element.29) | data formatting | bytes 196608
  81.5 1.5 %copy.17 = f32[8,24,128]{2,1,0:T(8,128)} copy(f32[8,24,128]{2,1,0:T(8,128)} %get-tuple-element.30) | data formatting | bytes 196608
  (3 shorter events, 0.0 us)
Async XLA Ops:
  2.5 3.0 %collective-permute-start.1 = (f32[8,3,24,128]{3,2,0,1:T(8,128)S(1)}, f32[8,3,24,128]{3,2,0,1:T(8,128)S(1)}, u32[]{:S(2)}, u32[]{:S(2)}) collective-permute-start(f32[8,3,24,128]{3,2,0,1:T(8,128)S(1)} %pad_maximum_fusion.3), channel_id=1, source_target_pairs={{0,1},{1,0},{2,3},{3,2},{4,5},{5,4},{6,7},{7,6},{8,9},{9,8},{10,11... | collective-permute-start | bytes 884744 | tf_op jit(solution)/shard_map/ppermute | solution.py:73
  3.1 1.7 %collective-permute-start = (s32[8]{0:T(128)}, s32[8]{0:T(128)S(1)}, u32[]{:S(2)}, u32[]{:S(2)}) collective-permute-start(s32[8]{0:T(128)} %param.6), channel_id=1, source_target_pairs={{0,1},{1,0},{2,3},{3,2},{4,5},{5,4},{6,7},{7,6},{8,9},{9,8},{10,11... | collective-permute-start | bytes 104 | tf_op jit(solution)/shard_map/ppermute | solution.py:73
  6.5 15.5 %copy-start.1 = (f32[8,24,128]{2,1,0:T(8,128)S(1)}, f32[8,24,128]{2,1,0:T(8,128)}, u32[]{:S(2)}) copy-start(f32[8,24,128]{2,1,0:T(8,128)} %param.7) | copy-start | bytes 294916
  6.5 15.5 %copy-start.2 = (f32[8,24,128]{2,1,0:T(8,128)S(1)}, f32[8,24,128]{2,1,0:T(8,128)}, u32[]{:S(2)}) copy-start(f32[8,24,128]{2,1,0:T(8,128)} %param.4) | copy-start | bytes 294916
  6.6 14.2 %collective-permute-start.2 = (f32[16,3,9,128]{3,2,0,1:T(8,128)S(1)}, f32[16,3,9,128]{3,2,0,1:T(8,128)S(1)}, u32[]{:S(2)}, u32[]{:S(2)}) collective-permute-start(f32[16,3,9,128]{3,2,0,1:T(8,128)S(1)} %get-tuple-element.7), channel_id=1, source_target_pairs={{8,0},{16,8},{24,16},{9,1},{17,9},{25,17},{10,2},{18,10},{26,18},{... | collective-permute-start | bytes 663560 | tf_op jit(solution)/shard_map/ppermute | solution.py:65
  7.9 14.1 %collective-permute-start.3 = (f32[16,3,9,128]{3,2,0,1:T(8,128)S(1)}, f32[16,3,9,128]{3,2,0,1:T(8,128)S(1)}, u32[]{:S(2)}, u32[]{:S(2)}) collective-permute-start(f32[16,3,9,128]{3,2,0,1:T(8,128)S(1)} %get-tuple-element.8), channel_id=1, source_target_pairs={{0,8},{8,16},{16,24},{1,9},{9,17},{17,25},{2,10},{10,18},{18,26},{... | collective-permute-start | bytes 663560 | tf_op jit(solution)/shard_map/ppermute | solution.py:65
  22.0 0.8 copy-start
  24.3 9.2 %collective-permute-start.4 = (f32[16,3,48,9]{2,0,3,1:T(8,128)}, f32[16,3,48,9]{2,0,3,1:T(8,128)S(1)}, u32[]{:S(2)}, u32[]{:S(2)}) collective-permute-start(f32[16,3,48,9]{2,0,3,1:T(8,128)} %copy.10), channel_id=1, source_target_pairs={{2,0},{4,2},{6,4},{3,1},{5,3},{7,5},{10,8},{12,10},{14,12},{11,9},... | collective-permute-start | bytes 248840 | tf_op jit(solution)/shard_map/ppermute | solution.py:65
  26.0 8.3 %collective-permute-start.5 = (f32[16,3,48,9]{2,0,3,1:T(8,128)S(1)}, f32[16,3,48,9]{2,0,3,1:T(8,128)}, u32[]{:S(2)}, u32[]{:S(2)}) collective-permute-start(f32[16,3,48,9]{2,0,3,1:T(8,128)S(1)} %copy.11), channel_id=1, source_target_pairs={{0,2},{2,4},{4,6},{1,3},{3,5},{5,7},{8,10},{10,12},{12,14},{9,11},... | collective-permute-start | bytes 248840 | tf_op jit(solution)/shard_map/ppermute | solution.py:65
  31.9 3.8 %copy-start.3 = (f32[256]{0:T(256)S(1)}, f32[256]{0:T(256)}, u32[]{:S(2)}) copy-start(f32[256]{0:T(256)} %pad.8.clone) | copy-start | bytes 3076

commit v4 on v3

--- a/solution.py
+++ b/solution.py
@@ -123,9 +123,13 @@
     SLOT[tuple(-o for o in _offset)] = (_column, 2 * _column + 1)
 
 
-def grid_kernel(extent, sizes, table, mask, potential, source, phi, residual,
+def grid_kernel(extent, sizes, local, table, mask_in, potential_in, source_in, phi, residual,
                 basis, scale, dots, weights, spare, first, second, jac,
-                own_row, early, final_row, late, sends, early_recv, late_recv):
+                own_row, early, final_row, late, sends, early_recv, late_recv, *extra):
+    mask, potential, source = mask_in, potential_in, source_in
+    if local:
+        fields, pack, from_after, from_before, face_send, face_recv = extra
+        mask, potential, source = fields.at[0], fields.at[1], fields.at[2]
     planes, rows, lanes = mask.shape
     nz, nx, ny = extent
     held = jac.shape[1]
@@ -186,10 +190,10 @@
     cells = jnp.zeros((1, ny), jnp.float32)
     injected = jnp.zeros((1, ny), jnp.float32)
     for plane in range(nz):
-        own_inside = jnp.where(mask[plane, 0:nx, 0:ny] > 0.0, 1.0, 0.0)
+        own_inside = jnp.where(mask_in[plane, 0:nx, 0:ny] > 0.0, 1.0, 0.0)
         cells = cells + jnp.sum(own_inside, axis=0, keepdims=True)
         injected = injected + jnp.sum(
-            own_inside * source[plane, 0:nx, 0:ny], axis=0, keepdims=True
+            own_inside * source_in[plane, 0:nx, 0:ny], axis=0, keepdims=True
         )
     cells = jnp.sum(cells, axis=1, keepdims=True)
     injected = jnp.sum(injected, axis=1, keepdims=True)
@@ -256,10 +260,98 @@
 
         return carry
 
-    lax.fori_loop(0, planes // 2, setup, 0)
-    pl.semaphore_wait(barrier, peers - 1)
-    spread(own_row, early, early_recv)
-    lax.fori_loop(planes // 2, planes, setup, 0)
+    def faces(axis, moves):
+        size = sizes[AXES.index(axis)]
+        place = lax.axis_index(axis)
+        copies = []
+        for slot, step, src, dst in moves:
+            copy = pltpu.make_async_remote_copy(
+                src_ref=src, dst_ref=dst, send_sem=face_send.at[slot],
+                recv_sem=face_recv.at[slot], device_id={axis: place + step},
+                device_id_type=pl.DeviceIdType.MESH,
+            )
+            copies.append((copy, step))
+            pl.when((place + step >= 0) & (place + step < size))(copy.start)
+        for copy, step in copies:
+            pl.when((place - step >= 0) & (place - step < size))(copy.wait_recv)
+            pl.when((place + step >= 0) & (place + step < size))(copy.wait_send)
+
+    if local:
+        inputs = (mask_in, potential_in, source_in)
+        first_x, last_x = lax.axis_index("gx") == 0, lax.axis_index("gx") == sizes[0] - 1
+        first_y, last_y = lax.axis_index("gy") == 0, lax.axis_index("gy") == sizes[1] - 1
+
+        @pl.when(last_x)
+        def _():
+            fields[:, 0:nz, nx : nx + 16, 0:ny] = jnp.zeros((3, nz, 16, ny), jnp.float32)
+
+        @pl.when(first_x)
+        def _():
+            fields[:, 0:nz, nx + 16 : nx + 32, 0:ny] = jnp.zeros((3, nz, 16, ny), jnp.float32)
+
+        @pl.when(last_y)
+        def _():
+            from_after[...] = jnp.zeros(from_after.shape, jnp.float32)
+
+        @pl.when(first_y)
+        def _():
+            from_before[...] = jnp.zeros(from_before.shape, jnp.float32)
+
+        for index, ref in enumerate(inputs):
+            fields[index, 0:nz, 0:nx, 0:ny] = ref[...]
+        pl.semaphore_wait(barrier, peers - 1)
+        spread(own_row, early, early_recv)
+        moves = []
+        for index, ref in enumerate(inputs):
+            to = fields.at[index, pl.ds(0, nz)]
+            moves.append(
+                (2 * index, 1, ref.at[:, pl.ds(nx - 16, 16)],
+                 to.at[:, pl.ds(nx + 16, 16), pl.ds(0, ny)])
+            )
+            moves.append(
+                (2 * index + 1, -1, ref.at[:, pl.ds(0, 16)],
+                 to.at[:, pl.ds(nx, 16), pl.ds(0, ny)])
+            )
+        faces("gx", moves)
+        column = lax.broadcasted_iota(jnp.int32, (rows, ny), 1)
+
+        def packing(plane, carry):
+            one = pltpu.roll(fields[1, plane, :, 0:ny], 32, 1)
+            two = pltpu.roll(fields[2, plane, :, 0:ny], 64, 1)
+            value = fields[0, plane, :, 0:ny]
+            value = jnp.where((column >= 23) & (column < 41), one, value)
+            pack[plane] = jnp.where((column >= 55) & (column < 73), two, value)
+            return carry
+
+        lax.fori_loop(0, nz, packing, 0)
+        faces("gy", [(6, 1, pack, from_before), (7, -1, pack, from_after)])
+
+        def unpacking(plane, carry):
+            for index in range(3):
+                after, before = from_after[plane], from_before[plane]
+                if index:
+                    after = pltpu.roll(after, ny - 32 * index, 1)
+                    before = pltpu.roll(before, ny - 32 * index, 1)
+                fields[index, plane, :, ny : 2 * ny] = jnp.where(
+                    column < DEPTH, after, jnp.where(column >= ny - DEPTH, before, 0.0)
+                )
+            return carry
+
+        lax.fori_loop(0, nz, unpacking, 0)
+        side = lax.axis_index("gz")
+        swap = pltpu.make_async_remote_copy(
+            src_ref=fields.at[:, pl.ds(0, nz)], dst_ref=fields.at[:, pl.ds(nz, nz)],
+            send_sem=face_send.at[8], recv_sem=face_recv.at[8],
+            device_id={"gz": 1 - side}, device_id_type=pl.DeviceIdType.MESH,
+        )
+        swap.start()
+        swap.wait()
+        lax.fori_loop(0, planes, setup, 0)
+    else:
+        lax.fori_loop(0, planes // 2, setup, 0)
+        pl.semaphore_wait(barrier, peers - 1)
+        spread(own_row, early, early_recv)
+        lax.fori_loop(planes // 2, planes, setup, 0)
     totals = collect(own_row, early, early_recv)
     count = pick(totals, 0)
     mean_rhs = pick(totals, 1) / count
@@ -383,10 +475,21 @@
     extent = tissue_mask.shape
     nz = extent[0]
     labels = tissue_mask.astype(jnp.float32)
-    packed = jnp.stack([labels, potential, source], axis=1)
-    packed = framed(packed, "gz", 0, 1)
-    packed = framed(packed, "gx", 2, 8)
-    packed = framed(packed, "gy", 3, 128)
+    sizes = tuple(lax.axis_size(axis) for axis in AXES)
+    local = (
+        sizes[2] == 2 and nz <= DEPTH and extent[1] % 8 == 0 and extent[1] >= 16
+        and extent[2] == 128
+    )
+    if local:
+        operands = (labels, potential, source)
+        frame = (2 * nz, extent[1] + 32, 2 * extent[2])
+    else:
+        packed = jnp.stack([labels, potential, source], axis=1)
+        packed = framed(packed, "gz", 0, 1)
+        packed = framed(packed, "gx", 2, 8)
+        packed = framed(packed, "gy", 3, 128)
+        operands = (packed[:, 0], packed[:, 1], packed[:, 2])
+        frame = operands[0].shape
     layers = framed(layer_index, "gz", 0, 1)
     planes = layers.shape[0]
     selector = (layers[:, None] == jnp.arange(LAYERS, dtype=jnp.int32)[None, :]).astype(
@@ -406,19 +509,22 @@
         place = (lax.axis_index("gz") * nz + jnp.arange(planes)) % planes
         link = (place + 1 < planes).astype(jnp.float32)[:, None]
     table = jnp.concatenate([table, link], axis=1)
-    frame = (planes,) + packed.shape[2:]
     smem = pl.BlockSpec(memory_space=pltpu.SMEM)
     vmem = pl.BlockSpec(memory_space=pltpu.VMEM)
     compact = frame
     if extent[1] % 8 == 0 and ITERS % 8 == 0 and frame[1] > extent[1] + 2 * ITERS:
         compact = (planes, extent[1] + 2 * ITERS, frame[2])
-    sizes = tuple(lax.axis_size(axis) for axis in AXES)
+    strip = pltpu.VMEM((nz,) + (frame[1], extent[2]), jnp.float32)
+    extra = []
+    if local:
+        extra = [pltpu.VMEM((3,) + frame, jnp.float32), strip, strip, strip]
+        extra += [pltpu.SemaphoreType.DMA((9,))] * 2
     peers = math.prod(sizes)
     row = pltpu.VMEM((1, 128), jnp.float32)
     gathered = pltpu.VMEM((peers, 1, 128), jnp.float32)
     return tuple(
         pl.pallas_call(
-            functools.partial(grid_kernel, extent, sizes),
+            functools.partial(grid_kernel, extent, sizes, local),
             out_shape=(jax.ShapeDtypeStruct(extent, jnp.float32),) * 2,
             in_specs=[smem, vmem, vmem, vmem],
             out_specs=(vmem, vmem),
@@ -430,11 +536,12 @@
             ]
             + [pltpu.VMEM(compact, jnp.float32)] * 4
             + [row, gathered, row, gathered]
-            + [pltpu.SemaphoreType.DMA((peers,))] * 3,
+            + [pltpu.SemaphoreType.DMA((peers,))] * 3
+            + extra,
             compiler_params=pltpu.CompilerParams(
                 vmem_limit_bytes=60 * 1024 * 1024, collective_id=0, has_side_effects=True
             ),
-        )(table, packed[:, 0], packed[:, 1], packed[:, 2])
+        )(table, *operands)
     )
 
 

time: 83.5 us -> 68.4 us (0.82)
  Pallas kernels: 41.3 us -> 60.6 us
  starting transfers between devices: 14 us -> 0.56 us
  waiting for transfers between devices: 10.4 us -> 0.01 us
  local copies, waits for them, and re-layouts: 9.65 us -> 2.87 us
  other arithmetic: 6.8 us -> 3.19 us
    pallas_call x1, Pallas kernels: 41.3 us -> 60.6 us  [body(): pl.pallas_call(functools.partial(grid_kernel, extent, sizes, local), out_...]
    ppermute x4 -> x0, starting transfers between devices: 13.4 us -> none  [shifted(): return lax.ppermute(value, axis, pairs)]
    ppermute x4 -> x0, waiting for transfers between devices: 10.4 us -> none  [shifted(): return lax.ppermute(value, axis, pairs)]
    slice x4 -> x0, local copies, waits for them, and re-layouts: 2 us -> none  [the longest x3 1.56 us: framed(): lax.slice_in_dim(value, 0, width, axis=dim)]
    another operation x2 -> x0, other arithmetic: 1.86 us -> none  [body(): packed = jnp.stack([labels, potential, source], axis=1)]
    ppermute x2 -> x0, local copies, waits for them, and re-layouts: 1.82 us -> none  [shifted(): return lax.ppermute(value, axis, pairs)]
    concatenate x2 -> x0, other arithmetic: 1.68 us -> none  [framed(): return jnp.concatenate([value] + after + middle + before, axis=dim)]
    concatenate x2 -> x1, other arithmetic: 1.71 us -> 0.07 us  [framed(): return jnp.concatenate([value, other], axis=dim)]
  transfers between devices with their start and end apart: 6 -> 1, of which waited for: 4 -> 0; matrix products, arithmetic and copies ran while one was open for 5% -> 4% of each run, Pallas kernels for 0% -> 0%
where the time goes in v4:
time: 68.4 us; the launch traced here: 68.1 us
  Pallas kernels  60.6 us (89%)
  other arithmetic  3.19 us (5%)
  local copies, waits for them, and re-layouts  2.87 us (4%)
  between operations  0.7 us (1%)
    pallas_call x1, Pallas kernels, body(): pl.pallas_call(functools.partial(grid_kernel, extent, sizes, local), out_...  60.6 us
    unnamed x6, local copies, waits for them, and re-layouts  2.8 us
    convert_element_type x1, other arithmetic, body(): labels = tissue_mask.astype(jnp.float32)  1.54 us
  transfers between devices with their start and end apart: 1, of which 0 were waited for; matrix products, arithmetic and copies ran while one was open for 4% of the time, Pallas kernels for 0%

profile of v4, /device:TPU:0, one launch (start us, length us, event | category | flops | bytes accessed | tf_op | source)
XLA Modules:
  0.0 68.1 jit_solution(7517303125009621998)
XLA Ops:
  0.6 0.6 collective-permute-start
  1.2 0.1 broadcast_maximum_fusion.4
  1.3 0.1 broadcast_maximum_fusion.2
  1.4 0.1 broadcast_maximum_fusion
  1.5 0.1 negate_maximum_fusion.5
  1.6 0.1 negate_maximum_fusion.3
  1.7 0.1 negate_maximum_fusion.2
  1.8 0.1 negate_maximum_fusion
  1.9 0.1 fusion.21
  2.0 0.1 fusion.11
  2.1 1.5 %convert_element_type.15.mask_in = f32[8,24,128]{2,1,0:T(8,128)} convert(s32[8,24,128]{2,1,0:T(8,128)} %param.5) | non-fusion elementwise | flops 24576 | bytes 196608 | tf_op jit(solution)/shard_map/convert_element_type | solution.py:477
  3.7 0.0 copy-start.1
  3.7 0.1 concatenate.10
  3.7 0.0 collective-permute-done
  3.7 0.6 copy-done.1
  4.3 0.1 pad_add_fusion
  4.4 0.2 fusion.7
  4.6 0.7 %pad_maximum_fusion.table = f32[16,19]{1,0:T(8,128)} fusion(f32[16,1]{1,0:T(8,128)S(1)} %fusion.5, f32[16,18]{1,0:T(8,128)S(1)} %fusion.7), kind=kLoop, calls=%fused_computation.6 | loop fusion | flops 304 | bytes 2432 | tf_op jit(solution)/shard_map/concatenate | solution.py:511
  5.3 60.6 %shard_map.59 = (f32[8,24,128]{2,1,0:T(8,128)}, f32[8,24,128]{2,1,0:T(8,128)}) custom-call(f32[16,19]{1,0:T(8,128)} %pad_maximum_fusion.table, f32[8,24,128]{2,1,0:T(8,128)} %convert_element_type.15.mask_in, f32[8,24,128]{2,1,0:T(8,128)} %potential_in.1, f32[8,24,128]{2,1,0:T(8,128)} %source_in.1), custom_call_target="tpu_custom_call" | custom-call | tf_op jit(solution)/shard_map/pallas_call | solution.py:526
  65.9 0.0 copy-start
  65.9 1.6 %copy.8 = f32[8,24,128]{2,1,0:T(8,128)} copy(f32[8,24,128]{2,1,0:T(8,128)} %get-tuple-element.22) | data formatting | bytes 196608
  67.5 0.0 copy-done
  67.5 0.6 copy.9
  (1 shorter events, 0.0 us)
Async XLA Ops:
  0.6 3.1 %collective-permute-start = (s32[8]{0:T(128)}, s32[8]{0:T(128)S(1)}, u32[]{:S(2)}, u32[]{:S(2)}) collective-permute-start(s32[8]{0:T(128)} %param.6), channel_id=1, source_target_pairs={{0,1},{1,0},{2,3},{3,2},{4,5},{5,4},{6,7},{7,6},{8,9},{9,8},{10,11... | collective-permute-start | bytes 104 | tf_op jit(solution)/shard_map/ppermute | solution.py:73
  3.7 0.7 copy-start.1
  65.9 1.6 %copy-start = (f32[8,24,128]{2,1,0:T(8,128)S(1)}, f32[8,24,128]{2,1,0:T(8,128)}, u32[]{:S(2)}) copy-start(f32[8,24,128]{2,1,0:T(8,128)} %get-tuple-element.23) | copy-start | bytes 294916
